TPU v7x, 32 devices: a whole 2x2x4 slice. The times are simulated.
32 devices in a mesh: tp: 4 (over z), dp: 8 (over y, x, core).
Axes of the slice: x: 2, y: 2, z: 4, core: 2. Of those that a mesh axis runs over, the one named last changes fastest.
Arguments:
- design: float32 [65536, 1536], P('dp', 'tp')
- target: float32 [65536], P('dp')
- ridge: float32 [], replicated
Outputs:
- output 1: float32 [1536], replicated
- output 2: float32 [65536], P('dp')
All inputs are finite; a program needn't handle non-finite values.
Results may differ from a plain program's by a relative error of at most 0.001.
Values sent between devices are 32-bit elements.
A program may use at most 1 GiB of HBM per device.

v0:
```python
import jax
import jax.numpy as jnp
from jax import lax
from jax.sharding import PartitionSpec as P

HIGHEST = lax.Precision.HIGHEST
CONTRACT_ROWS = (((0,), (0,)), ((), ()))


def solve_factored(chol_low, rhs_vec):
    half_solve = lax.linalg.triangular_solve(chol_low, rhs_vec[:, None], left_side=True, lower=True)
    return lax.linalg.triangular_solve(chol_low, half_solve, left_side=True, lower=True, transpose_a=True)[:, 0]


def solution(mesh):
    col_ways = mesh.shape['tp']

    def local_fit(design_blk, target_blk, ridge):
        rows_dev, cols_dev = design_blk.shape
        features = cols_dev * col_ways
        sub_rows = rows_dev // col_ways
        col_index = lax.axis_index('tp')
        row_panel = lax.all_to_all(design_blk, 'tp', 0, 1, tiled=True)
        target_part = lax.dynamic_slice_in_dim(target_blk, col_index * sub_rows, sub_rows)
        gram_part = lax.dot_general(row_panel, row_panel, CONTRACT_ROWS, precision=HIGHEST, preferred_element_type=jnp.float32)
        moment_part = lax.dot_general(row_panel, target_part, CONTRACT_ROWS, precision=HIGHEST, preferred_element_type=jnp.float32)
        gram_mat = lax.psum(gram_part, ('tp', 'dp'))
        moment_vec = lax.psum(moment_part, ('tp', 'dp'))
        chol_low = jnp.linalg.cholesky(gram_mat + ridge * jnp.eye(features, dtype=jnp.float32))
        coeffs = solve_factored(chol_low, moment_vec)
        coeff_blk = lax.dynamic_slice_in_dim(coeffs, col_index * cols_dev, cols_dev)
        part_fit = jnp.dot(design_blk, coeff_blk, precision=HIGHEST, preferred_element_type=jnp.float32)
        fitted = lax.psum(part_fit, 'tp')
        return coeffs, target_blk - fitted

    return jax.shard_map(local_fit, mesh=mesh, in_specs=(P('dp', 'tp'), P('dp'), P()), out_specs=(P(), P('dp')), check_vma=False)
```

profile of v0, /device:TPU:0, one launch (start us, length us, event | category | flops | bytes accessed | tf_op | source)
XLA Modules:
  0.0 1175.6 jit_solution(3764410193096420478)
XLA Ops:
  7.2 283.3 %all_to_all.19 = f32[4,2048,384]{2,1,0:T(8,128)} all-to-all(f32[4,2048,384]{2,1,0:T(8,128)} %bitcast.523), channel_id=1, replica_groups=mesh['tp'=4,'dp'=8] {'tp'}, dimensions={0} | all-to-all | bytes 25165824 | tf_op jit(solution)/shard_map/all_to_all | solution.py:23
  290.5 12.6 %copy.57 = f32[2048,4,384]{0,2,1:T(8,128)} copy(f32[2048,4,384]{2,0,1:T(8,128)} %bitcast.526) | data formatting | bytes 25165824 | tf_op jit(solution)/shard_map/all_to_all | solution.py:23
  303.1 67.4 %fusion.191 = f32[1536,1536]{0,1:T(8,128)} fusion(f32[2048,1536]{0,1:T(8,128)} %bitcast.524), kind=kOutput, calls=%fused_computation.420 | convolution fusion | flops 57982058496 | bytes 22020096 | tf_op jit(solution)/shard_map/dot_general | solution.py:25
  371.3 13.1 %convolution_reduce_fusion = f32[1536]{0:T(1024)S(1)} fusion(f32[2048,1]{0,1:T(1,128)S(1)} %bitcast.528, f32[2048,1536]{0,1:T(8,128)} %bitcast.525), kind=kOutput, calls=%fused_computation.45 | convolution fusion | flops 37748736 | bytes 12597248 | tf_op jit(solution)/shard_map/dot_general | solution.py:26
  384.4 43.7 %psum.22 = f32[1536]{0:T(1024)S(1)} all-reduce(f32[1536]{0:T(1024)S(1)} %convolution_reduce_fusion), channel_id=1, replica_groups=mesh['tp'=4,'dp'=8] {'tp','dp'}, use_global_device_ids=true, to_apply=%region_25.26 | all-reduce | flops 1536 | bytes 12288 | tf_op jit(solution)/shard_map/psum | solution.py:28
  428.1 136.2 %all-reduce.3.cloned.1.call-done = f32[1536,1536]{0,1:T(8,128)} async-done(((f32[1536,1536]{0,1:T(8,128)}), f32[1536,1536]{0,1:T(8,128)}) %all-reduce.3.cloned.1.call-update) | async-done | bytes 9437200 | tf_op jit(solution)/shard_map/psum | solution.py:27
  582.5 12.3 %fusion = f32[1536,1536]{1,0:T(8,128)} fusion(f32[1536,1536]{1,0:T(8,128)} %copy.59, f32[1536,1536]{0,1:T(8,128)} %all-reduce.3.cloned.1.call-done, f32[]{:T(128)S(6)} %copy.237), kind=kLoop, calls=%fused_computation.4 | loop fusion | flops 11796480 | bytes 28311556 | tf_op jit(solution)/shard_map/jit(cholesky)/div | solution.py:29
  595.6 11.7 cholesky.340
  621.2 12.1 %cholesky.361 = f32[128,128]{1,0:T(8,128)S(1)} custom-call(f32[128,128]{1,0:T(8,128)S(1)} %cholesky.893), custom_call_target="Cholesky" | custom-call | tf_op jit(solution)/shard_map/jit(cholesky)/cholesky | solution.py:29
  652.3 11.7 cholesky.384
  681.0 11.7 cholesky.713
  710.2 11.7 cholesky.732
  740.0 11.7 cholesky.752
  769.3 11.9 %cholesky.772 = f32[128,128]{1,0:T(8,128)S(1)} custom-call(f32[128,128]{1,0:T(8,128)S(1)} %cholesky.918), custom_call_target="Cholesky" | custom-call | tf_op jit(solution)/shard_map/jit(cholesky)/cholesky | solution.py:29
  798.6 11.9 %cholesky.792 = f32[128,128]{1,0:T(8,128)S(1)} custom-call(f32[128,128]{1,0:T(8,128)S(1)} %cholesky.923), custom_call_target="Cholesky" | custom-call | tf_op jit(solution)/shard_map/jit(cholesky)/cholesky | solution.py:29
  827.5 11.7 cholesky.812
  840.0 10.2 custom-call.104
  856.0 11.7 cholesky.832
  883.2 11.7 cholesky.852
  909.2 11.7 cholesky.870
  945.3 36.5 %while.1 = (s32[]{:T(128)}, f32[1536,1536]{0,1:T(8,128)}, s32[12,2]{0,1:T(2,128)S(1)}, f32[12,128,128]{2,1,0:T(8,128)S(1)}, s32[]{:T(128)}) while((s32[]{:T(128)}, f32[1536,1536]{0,1:T(8,128)}, s32[12,2]{0,1:T(2,128)S(1)}, f32[12,128,128]{2,1,0:T(8,128)S(1)}, s32[]{:T(128)}) %tuple.101), condition=%wide.while_cond, body=%wide.while_body.sunk | while | flops 2 | bytes 393329 | solution.py:12
  981.8 117.9 %custom-call.107 = f32[12,128,128]{1,2,0:T(8,128)S(1)} custom-call(f32[12,128,128]{2,1,0:T(8,128)S(1)} %get-tuple-element.9), custom_call_target="InvertDiagBlocksLowerTriangular" | custom-call | tf_op jit(solution)/shard_map/triangular_solve | solution.py:12
  1136.2 13.3 %fusion.174 = f32[1,8192]{1,0:T(1,128)S(1)} fusion(f32[8192,384]{1,0:T(8,128)} %param.3, f32[1536,1]{0,1:T(1,128)S(1)} %constant_dynamic-update-slice_fusion.112, s32[]{:T(128)S(6)} %select_n.12), kind=kOutput, calls=%fused_computation.389 | convolution fusion | flops 37748736 | bytes 12617220 | tf_op jit(solution)/shard_map/dot_general | solution.py:32
  1149.5 18.1 %psum.23 = f32[8192]{0:T(1024)S(1)} all-reduce(f32[8192]{0:T(1024)S(1)} %bitcast.527), channel_id=1, replica_groups=mesh['tp'=4,'dp'=8] {'tp'}, use_global_device_ids=true, to_apply=%region_26.27 | all-reduce | flops 8192 | bytes 65536 | tf_op jit(solution)/shard_map/psum | solution.py:33
  (273 shorter events, 282.4 us)
Async XLA Ops:
  7.2 557.2 %all-reduce.3.cloned.1.call-start = ((), (), s32[]{:S(2)}) async-start(), calls=%async_computation.1 | async-start | bytes 18874368 | tf_op jit(solution)/shard_map/psum | solution.py:27
  370.5 0.8 copy-start.1
  645.3 3.7 copy-start
Sparse Core Ops, SparseCore 0:
  370.6 193.6 all-reduce.2
where the time goes:
time: 1190 us; the launch traced here: 1180 us
  other arithmetic  406 us (34%)
  blocking collectives  345 us (29%)
  matrix products  191 us (16%)
  waiting for transfers between devices  136 us (11%)
  local copies, waits for them, and re-layouts  73.1 us (6%)
  between operations  23.3 us (2%)
    all_to_all x1, blocking collectives, local_fit(): row_panel = lax.all_to_all(design_blk, 'tp', 0, 1, tiled=True)  283 us
    another operation x46, other arithmetic, local_fit(): jnp.linalg.cholesky(gram_mat + ridge * jnp.eye(features, dtype=jnp.float32))  258 us
    psum x1, waiting for transfers between devices, local_fit(): gram_mat = lax.psum(gram_part, ('tp', 'dp'))  136 us
    another operation x4, other arithmetic, solve_factored(): lax.linalg.triangular_solve(chol_low, half_solve, left_side=True, lower=T...  127 us
    dot_general x1, matrix products, local_fit(): lax.dot_general(row_panel, row_panel, CONTRACT_ROWS, precision=HIGHEST, p...  67.4 us
    another operation x22, matrix products, local_fit(): jnp.linalg.cholesky(gram_mat + ridge * jnp.eye(features, dtype=jnp.float32))  62.7 us
    psum x1, blocking collectives, local_fit(): moment_vec = lax.psum(moment_part, ('tp', 'dp'))  43.7 us
    another operation x60, local copies, waits for them, and re-layouts  36.1 us
  transfers between devices with their start and end apart: 1, of which 1 were waited for; matrix products, arithmetic and copies ran while one was open for 1% of the time, Pallas kernels for 0%

commit v1 on v0

v1 whole, which is shorter than its diff:
```python
import functools
import jax, jax.numpy as jnp
from jax import lax
from jax.experimental import pallas as pl
from jax.experimental.pallas import tpu as pltpu
from jax.sharding import PartitionSpec as P

HIGHEST = lax.Precision.HIGHEST
F32 = jnp.float32
SUB, HALF, PANEL = 16, 128, 256


def dot(a, b, dims=((1,), (0,))):
    return lax.dot_general(a, b, (dims, ((), ())), precision=HIGHEST, preferred_element_type=F32)


def micro_rows(left, right, col0):
    rows = lax.broadcasted_iota(jnp.int32, (SUB, HALF), 0)
    cols = [jnp.broadcast_to(left[:, col0 + c:col0 + c + 1], (SUB, HALF)) for c in range(SUB)]
    pivots = cols[0]
    for p in range(SUB):
        inv = 1.0 / cols[p][p:p + 1, :]
        fac = jnp.where(rows > p, cols[p] * inv, 0.0)
        for c in range(p + 1, SUB):
            cols[c] = cols[c] - fac * cols[c][p:p + 1, :]
        left = left - fac * left[p:p + 1, :]
        right = right - fac * right[p:p + 1, :]
        pivots = jnp.where(rows == p, cols[p], pivots)
    scale = lax.rsqrt(pivots)
    return left * scale, right * scale


def invert_factor(work, inv_ref, row0):
    for m in range(HALF // SUB):
        r = m * SUB
        left, right = micro_rows(work[r:r + SUB, :HALF], work[r:r + SUB, HALF:], r)
        inv_ref[row0 + r:row0 + r + SUB, row0:row0 + HALF] = right
        if r + SUB < HALF:
            both = jnp.concatenate([left, right], axis=1)
            upd = dot(left, both, ((0,), (0,)))
            work[r + SUB:, :] = work[r + SUB:, :] - upd[r + SUB:, :]


def eye(n):
    return jnp.where(lax.broadcasted_iota(jnp.int32, (n, n), 0) == lax.broadcasted_iota(jnp.int32, (n, n), 1), 1.0, 0.0).astype(F32)


def factor(up, inv, work, n, width):
    panels = n // PANEL

    def step(k, _):
        r0 = pl.multiple_of(k * PANEL, PANEL)
        winv = inv.at[k]
        winv[...] = jnp.zeros((PANEL, PANEL), F32)
        work[:, :HALF] = up[pl.ds(r0, HALF), pl.ds(r0, HALF)]
        work[:, HALF:] = eye(HALF)
        invert_factor(work, winv, 0)
        w1 = winv[:HALF, :HALF]
        u12 = dot(w1, up[pl.ds(r0, HALF), pl.ds(r0 + HALF, HALF)])
        work[:, :HALF] = up[pl.ds(r0 + HALF, HALF), pl.ds(r0 + HALF, HALF)] - dot(u12, u12, ((0,), (0,)))
        work[:, HALF:] = eye(HALF)
        t = dot(u12, w1, ((0,), (0,)))
        invert_factor(work, winv, HALF)
        w2 = winv[HALF:, HALF:]
        winv[HALF:, :HALF] = -dot(w2, t)
        for kk in range(panels):
            @pl.when(k == kk)
            def _():
                a, b = kk * PANEL, (kk + 1) * PANEL
                up[a:b, b:] = dot(winv[...], up[a:b, b:])
                for i in range(kk + 1, panels):
                    c = i * PANEL
                    up[c:c + PANEL, c:] = up[c:c + PANEL, c:] - dot(up[a:b, c:c + PANEL], up[a:b, c:], ((0,), (0,)))
        return 0

    lax.fori_loop(0, panels, step, 0)


def back_solve(up, inv, x_ref, n, rhs_col):
    panels = n // PANEL
    for k in range(panels - 1, -1, -1):
        a, b = k * PANEL, (k + 1) * PANEL
        v = up[a:b, rhs_col:rhs_col + 1]
        if b < n:
            v = v - jnp.sum(up[a:b, b:n] * x_ref[0:1, b:n], axis=1, keepdims=True)
        x_ref[0:1, a:b] = jnp.sum(inv[k] * v, axis=0, keepdims=True)


def solve_kernel(n, gram, x_ref, up, inv, work, sem):
    copy = pltpu.make_async_copy(gram, up, sem)
    copy.start()
    copy.wait()
    factor(up, inv, work, n, up.shape[1])
    back_solve(up, inv, x_ref, n, n)


def solve(gram_aug):
    n, width = gram_aug.shape
    return pl.pallas_call(
        functools.partial(solve_kernel, n),
        out_shape=jax.ShapeDtypeStruct((1, n), F32),
        in_specs=[pl.BlockSpec(memory_space=pl.ANY)],
        out_specs=pl.BlockSpec(memory_space=pltpu.VMEM),
        scratch_shapes=[
            pltpu.VMEM((n, width), F32),
            pltpu.VMEM((n // PANEL, PANEL, PANEL), F32),
            pltpu.VMEM((HALF, 2 * HALF), F32),
            pltpu.SemaphoreType.DMA,
        ],
        compiler_params=pltpu.CompilerParams(vmem_limit_bytes=48 * 1024 * 1024),
        cost_estimate=pl.CostEstimate(flops=int(n) ** 3 * 4, bytes_accessed=4 * n * width, transcendentals=0),
        name="factor_solve",
    )(gram_aug)


def solution(mesh):
    col_ways = mesh.shape['tp']

    def local_fit(design_blk, target_blk, ridge):
        rows_dev, cols_dev = design_blk.shape
        features = cols_dev * col_ways
        sub_rows = rows_dev // col_ways
        col_index = lax.axis_index('tp')
        row_panel = lax.all_to_all(design_blk, 'tp', 0, 1, tiled=True)
        target_part = lax.dynamic_slice_in_dim(target_blk, col_index * sub_rows, sub_rows)
        target_pad = jnp.pad(target_part[:, None], ((0, 0), (0, HALF - 1)))
        gram_part = dot(row_panel, jnp.concatenate([row_panel, target_pad], axis=1), ((0,), (0,)))
        gram_aug = lax.psum(gram_part, ('tp', 'dp'))
        row_id = lax.broadcasted_iota(jnp.int32, gram_aug.shape, 0)
        col_id = lax.broadcasted_iota(jnp.int32, gram_aug.shape, 1)
        coeffs = solve(jnp.where(row_id == col_id, gram_aug + ridge, gram_aug))[0]
        coeff_blk = lax.dynamic_slice_in_dim(coeffs, col_index * cols_dev, cols_dev)
        fitted = lax.psum(dot(design_blk, coeff_blk, ((1,), (0,))), 'tp')
        return coeffs, target_blk - fitted

    return jax.shard_map(local_fit, mesh=mesh, in_specs=(P('dp', 'tp'), P('dp'), P()), out_specs=(P(), P('dp')), check_vma=False)
```

time: 1190 us -> 713 us (0.60); the launches traced: 1180 us -> 712 us
  other arithmetic: 406 us -> 9.62 us
  waiting for transfers between devices: 136 us -> 473 us
  blocking collectives: 345 us -> 18.1 us
  matrix products: 191 us -> 92.5 us
  Pallas kernels: 0 us -> 85.6 us
  local copies, waits for them, and re-layouts: 73.1 us -> 12.6 us
    another operation x50 -> x0, other arithmetic: 385 us -> none  [the longest x46 258 us: local_fit(): jnp.linalg.cholesky(gram_mat + ridge * jnp.eye(features, dtype=jnp.float32))]
    all_to_all x1 -> x0, blocking collectives: 283 us -> none  [local_fit(): row_panel = lax.all_to_all(design_blk, 'tp', 0, 1, tiled=True)]
    all_to_all x0 -> x1, waiting for transfers between devices: none -> 274 us  [local_fit(): row_panel = lax.all_to_all(design_blk, 'tp', 0, 1, tiled=True)]
    another operation x68 -> x0, matrix products: 97.6 us -> none  [the longest x22 62.7 us: local_fit(): jnp.linalg.cholesky(gram_mat + ridge * jnp.eye(features, dtype=jnp.float32))]
    pallas_call x0 -> x1, Pallas kernels: none -> 85.6 us  [solve(): pl.pallas_call(functools.partial(solve_kernel, n), out_shape=jax.ShapeDty...]
    psum x1, waiting for transfers between devices: 136 us -> 198 us  [local_fit(): gram_aug = lax.psum(gram_part, ('tp', 'dp'))]
    another operation x106 -> x0, local copies, waits for them, and re-layouts: 46.2 us -> none
    psum x2 -> x1, blocking collectives: 61.8 us -> 18.1 us  [local_fit(): fitted = lax.psum(dot(design_blk, coeff_blk, ((1,), (0,))), 'tp')]
  transfers between devices with their start and end apart: 1 -> 2, of which waited for: 1 -> 2; matrix products, arithmetic and copies ran while one was open for 1% -> 0% of each run, Pallas kernels for 0% -> 0%
where the time goes in v1:
time: 713 us; the launch traced here: 712 us
  waiting for transfers between devices  473 us (66%)
  matrix products  92.5 us (13%)
  Pallas kernels  85.6 us (12%)
  blocking collectives  18.1 us (3%)
  between operations  14.7 us (2%)
  local copies, waits for them, and re-layouts  12.6 us (2%)
  other arithmetic  9.62 us (1%)
    all_to_all x1, waiting for transfers between devices, local_fit(): row_panel = lax.all_to_all(design_blk, 'tp', 0, 1, tiled=True)  274 us
    psum x1, waiting for transfers between devices, local_fit(): gram_aug = lax.psum(gram_part, ('tp', 'dp'))  198 us
    dot_general x2, matrix products, dot(): lax.dot_general(a, b, (dims, ((), ())), precision=HIGHEST, preferred_elem...  92.5 us
    pallas_call x1, Pallas kernels, solve(): pl.pallas_call(functools.partial(solve_kernel, n), out_shape=jax.ShapeDty...  85.6 us
    psum x1, blocking collectives, local_fit(): fitted = lax.psum(dot(design_blk, coeff_blk, ((1,), (0,))), 'tp')  18.1 us
  transfers between devices with their start and end apart: 2, of which 2 were waited for; matrix products, arithmetic and copies ran while one was open for 0% of the time, Pallas kernels for 0%

profile of v1, /device:TPU:0, one launch (start us, length us, event | category | flops | bytes accessed | tf_op | source)
XLA Modules:
  0.0 712.2 jit_solution(8047501205422205357)
XLA Ops:
  7.2 6.4 all-to-all-start
  13.6 0.0 all-reduce.3.cloned.1.call-start
  13.6 274.3 %all-to-all-done = f32[4,2048,384]{2,1,0:T(8,128)} async-done(((f32[4,2048,384]{2,1,0:T(8,128)}), f32[4,2048,384]{2,1,0:T(8,128)}, u32[]{:S(2)}, u32[]{:S(2)}) %all-to-all-start) | async-done | bytes 12582944 | tf_op jit(solution)/shard_map/all_to_all | solution.py:124
  287.8 0.0 dynamic-slice-start
  287.8 12.6 %copy.7 = f32[2048,4,384]{0,2,1:T(8,128)} copy(f32[2048,4,384]{2,0,1:T(8,128)} %bitcast.1) | data formatting | bytes 25165824 | tf_op jit(solution)/shard_map/all_to_all | solution.py:124
  300.5 0.0 dynamic-slice-done
  300.5 79.4 %fusion.3 = f32[1536,1664]{1,0:T(8,128)} fusion(f32[2048,1536]{0,1:T(8,128)} %bitcast.15, f32[2048,1]{0,1:T(1,128)S(1)} %bitcast.17), kind=kOutput, calls=%fused_computation.7 | convolution fusion | flops 62824120320 | bytes 22814720 | tf_op jit(solution)/shard_map/dot_general | solution.py:14
  379.9 0.0 all-reduce.3.cloned.1.call-update
  380.6 198.3 %all-reduce.3.cloned.1.call-done = f32[1536,1664]{1,0:T(8,128)} async-done(((f32[1536,1664]{1,0:T(8,128)}), f32[1536,1664]{1,0:T(8,128)}) %all-reduce.3.cloned.1.call-update) | async-done | bytes 10223632 | tf_op jit(solution)/shard_map/psum | solution.py:128
  578.9 8.4 %add_select_fusion.gram = f32[1536,1664]{1,0:T(8,128)} fusion(f32[1536,1664]{1,0:T(8,128)} %all-reduce.3.cloned.1.call-done, f32[]{:T(128)S(6)} %copy.11), kind=kLoop, calls=%fused_computation | loop fusion | flops 7667712 | bytes 20447236 | tf_op jit(solution)/shard_map/jit(_where)/select_n | solution.py:131
  587.3 85.6 %factor_solve.1 = f32[1,1536]{1,0:T(1,128)S(1)} custom-call(f32[1536,1664]{1,0:T(8,128)} %add_select_fusion.gram), custom_call_target="tpu_custom_call" | custom-call | flops 14495514624 | bytes 10223616 | tf_op jit(solution)/shard_map/factor_solve/pallas_call | solution.py:99
  672.9 0.0 copy-start
  672.9 0.6 reduce
  673.5 13.1 %fusion.6 = f32[1,8192]{1,0:T(1,128)S(1)} fusion(f32[8192,384]{1,0:T(8,128)} %param.3, f32[1,1536]{1,0:T(1,128)S(1)} %factor_solve.1, s32[]{:T(128)S(6)} %select_n.12), kind=kOutput, calls=%fused_computation.10 | convolution fusion | flops 37748736 | bytes 12617220 | tf_op jit(solution)/shard_map/dot_general | solution.py:14
  686.6 18.1 %psum.15 = f32[8192]{0:T(1024)S(1)} all-reduce(f32[8192]{0:T(1024)S(1)} %bitcast.16), channel_id=1, replica_groups=mesh['tp'=4,'dp'=8] {'tp'}, use_global_device_ids=true, to_apply=%region_1.2 | all-reduce | flops 8192 | bytes 65536 | tf_op jit(solution)/shard_map/psum | solution.py:133
  704.7 0.0 copy-done
  704.7 0.6 sub.3
Async XLA Ops:
  7.2 280.7 %all-to-all-start = ((f32[4,2048,384]{2,1,0:T(8,128)}), f32[4,2048,384]{2,1,0:T(8,128)}, u32[]{:S(2)}, u32[]{:S(2)}) async-start(f32[4,2048,384]{2,1,0:T(8,128)} %bitcast.14), calls=%async_computation | async-start | bytes 25165824 | tf_op jit(solution)/shard_map/all_to_all | solution.py:124
  13.6 565.4 %all-reduce.3.cloned.1.call-start = ((), (), s32[]{:S(2)}) async-start(), calls=%async_computation.1 | async-start | bytes 20447232 | tf_op jit(solution)/shard_map/psum | solution.py:128
  287.8 12.6 %dynamic-slice-start = ((f32[8192]{0:T(1024)}, s32[]{:T(128)}), f32[2048]{0:T(1024)S(1)}, s32[]{:S(2)}) async-start(f32[8192]{0:T(1024)} %param.4, s32[]{:T(128)} %select_n.10), calls=%async_computation.2 | async-start | bytes 16896 | tf_op jit(solution)/shard_map/dynamic_slice | solution.py:125
  672.9 31.9 %copy-start = (f32[8192]{0:T(1024)S(1)}, f32[8192]{0:T(1024)}, u32[]{:S(2)}) copy-start(f32[8192]{0:T(1024)} %param.4) | copy-start | bytes 98308
Sparse Core Ops, SparseCore 0:
  380.0 198.8 all-reduce.2

commit v2 on v1

v2 whole, which is shorter than its diff:
```python
import functools
import jax
import jax.numpy as jnp
from jax import lax
from jax.experimental import pallas as pl
from jax.experimental.pallas import tpu as pltpu
from jax.sharding import PartitionSpec as P

HIGHEST = lax.Precision.HIGHEST
F32 = jnp.float32
SUB, HALF, PANEL, BLOCK, EXTRA = 16, 128, 256, 384, 128
PAIR = 2 * BLOCK
MESH = pl.DeviceIdType.MESH
MIB = 1024 * 1024


def dot(a, b, dims=((1,), (0,))):
    return lax.dot_general(a, b, (dims, ((), ())), precision=HIGHEST, preferred_element_type=F32)


def micro_rows(left, right, col0):
    rows = lax.broadcasted_iota(jnp.int32, (SUB, HALF), 0)
    cols = [jnp.broadcast_to(left[:, col0 + c:col0 + c + 1], (SUB, HALF)) for c in range(SUB)]
    pivots = cols[0]
    for p in range(SUB):
        inv = 1.0 / cols[p][p:p + 1, :]
        fac = jnp.where(rows > p, cols[p] * inv, 0.0)
        for c in range(p + 1, SUB):
            cols[c] = cols[c] - fac * cols[c][p:p + 1, :]
        left = left - fac * left[p:p + 1, :]
        right = right - fac * right[p:p + 1, :]
        pivots = jnp.where(rows == p, cols[p], pivots)
    scale = lax.rsqrt(pivots)
    return left * scale, right * scale


def invert_factor(work, inv_ref, row0):
    for m in range(HALF // SUB):
        r = m * SUB
        left, right = micro_rows(work[r:r + SUB, :HALF], work[r:r + SUB, HALF:], r)
        inv_ref[row0 + r:row0 + r + SUB, row0:row0 + HALF] = right
        if r + SUB < HALF:
            both = jnp.concatenate([left, right], axis=1)
            upd = dot(left, both, ((0,), (0,)))
            work[r + SUB:, :] = work[r + SUB:, :] - upd[r + SUB:, :]


def eye(n):
    return jnp.where(lax.broadcasted_iota(jnp.int32, (n, n), 0) == lax.broadcasted_iota(jnp.int32, (n, n), 1), 1.0, 0.0).astype(F32)


def factor(up, inv, work, n):
    panels = n // PANEL

    def step(k, _):
        r0 = pl.multiple_of(k * PANEL, PANEL)
        winv = inv.at[k]
        winv[...] = jnp.zeros((PANEL, PANEL), F32)
        work[:, :HALF] = up[pl.ds(r0, HALF), pl.ds(r0, HALF)]
        work[:, HALF:] = eye(HALF)
        invert_factor(work, winv, 0)
        w1 = winv[:HALF, :HALF]
        u12 = dot(w1, up[pl.ds(r0, HALF), pl.ds(r0 + HALF, HALF)])
        work[:, :HALF] = up[pl.ds(r0 + HALF, HALF), pl.ds(r0 + HALF, HALF)] - dot(u12, u12, ((0,), (0,)))
        work[:, HALF:] = eye(HALF)
        t = dot(u12, w1, ((0,), (0,)))
        invert_factor(work, winv, HALF)
        w2 = winv[HALF:, HALF:]
        winv[HALF:, :HALF] = -dot(w2, t)
        for kk in range(panels):
            @pl.when(k == kk)
            def _():
                a, b = kk * PANEL, (kk + 1) * PANEL
                up[a:b, b:] = dot(winv[...], up[a:b, b:])
                for i in range(kk + 1, panels):
                    c = i * PANEL
                    up[c:c + PANEL, c:] = up[c:c + PANEL, c:] - dot(up[a:b, c:c + PANEL], up[a:b, c:], ((0,), (0,)))
        return 0

    lax.fori_loop(0, panels, step, 0)


def places():
    z, dp = lax.axis_index('tp'), lax.axis_index('dp')
    core, x, y = lax.rem(dp, 2), lax.rem(dp // 2, 2), dp // 4
    return z, dp, core, x, y


def z_peers(z):
    return (z + 1 - 2 * lax.rem(z, 2), z + 2 - 4 * (z // 2), 3 - z)


def reduce_kernel(rows, gather, part, out, acc, full, got_core, got_a, got_b, got_a2, got_b2, got_z, send_sem, recv_sem, out_sem):
    z, dp, core, x, y = places()
    half, quart, eighth, sixt = rows // 2, rows // 4, rows // 8, rows // 16
    core_peer = {'tp': z, 'dp': dp + 1 - 2 * core}
    x_peer = {'tp': z, 'dp': dp + 2 - 4 * x}
    y_peer = {'tp': z, 'dp': dp + 4 - 8 * y}
    z_peer = [{'tp': p, 'dp': dp} for p in z_peers(z)]
    peers = [core_peer, x_peer, y_peer] + z_peer
    barrier = pltpu.get_barrier_semaphore()
    for peer in peers:
        pl.semaphore_signal(barrier, inc=1, device_id=peer, device_id_type=MESH)
    pl.semaphore_wait(barrier, len(peers))
    count = [0]

    def start(src, dst, peer):
        i = count[0]
        count[0] += 1
        copy = pltpu.make_async_remote_copy(src_ref=src, dst_ref=dst, send_sem=send_sem.at[i], recv_sem=recv_sem.at[i], device_id=peer, device_id_type=MESH)
        copy.start()
        return copy

    def at(base, size):
        return pl.ds(pl.multiple_of(base, 8), size)

    own = core * half
    copy = start(part.at[at((1 - core) * half, half)], got_core, core_peer)
    copy.wait()
    acc[...] = part[at(own, half)] + got_core[...]
    copies = [start(acc.at[at((1 - x) * eighth, eighth)], got_a, x_peer), start(acc.at[at(quart + (1 - y) * eighth, eighth)], got_b, y_peer)]
    a1, b1 = x * eighth, quart + y * eighth
    copies[0].wait()
    acc[at(a1, eighth)] = acc[at(a1, eighth)] + got_a[...]
    copies[1].wait()
    acc[at(b1, eighth)] = acc[at(b1, eighth)] + got_b[...]
    copies = [start(acc.at[at(a1 + (1 - y) * sixt, sixt)], got_a2, y_peer), start(acc.at[at(b1 + (1 - x) * sixt, sixt)], got_b2, x_peer)]
    a2, b2 = a1 + y * sixt, b1 + x * sixt
    if gather:
        copies[0].wait()
        full[z, at(own + a2, sixt)] = acc[at(a2, sixt)] + got_a2[...]
        copies[1].wait()
        full[z, at(own + b2, sixt)] = acc[at(b2, sixt)] + got_b2[...]
        copies = []
        for piece in (a2, b2):
            ref = full.at[z, at(own + piece, sixt)]
            copies += [start(ref, ref, peer) for peer in z_peer]
        for copy in copies:
            copy.wait()
    else:
        copies[0].wait()
        acc[at(a2, sixt)] = acc[at(a2, sixt)] + got_a2[...]
        copies[1].wait()
        acc[at(b2, sixt)] = acc[at(b2, sixt)] + got_b2[...]
        share = sixt // 4
        copies = []
        for k, piece in enumerate((a2, b2)):
            for j, peer in enumerate(z_peer):
                copies.append(start(acc.at[at(piece + peer['tp'] * share, share)], got_z.at[2 * j + k], peer))
        for copy in copies:
            copy.wait()
        copies = []
        for k, piece in enumerate((a2, b2)):
            mine = piece + z * share
            full[0, at(own + mine, share)] = (acc[at(mine, share)] + got_z[k]) + (got_z[2 + k] + got_z[4 + k])
            ref = full.at[0, at(own + mine, share)]
            copies += [start(ref, ref, peer) for peer in z_peer]
        for copy in copies:
            copy.wait()
    for sizes in (((a2, sixt, y_peer), (b2, sixt, x_peer)), ((a1, eighth, x_peer), (b1, eighth, y_peer)), ((0, half, core_peer),)):
        copies = []
        for base, size, peer in sizes:
            ref = full.at[:, at(own + base, size)]
            copies.append(start(ref, ref, peer))
        for copy in copies:
            copy.wait()
    copy = pltpu.make_async_copy(full, out, out_sem)
    copy.start()
    copy.wait()


def reduce_all(part, gather, ident):
    rows = part.shape[0]
    slabs = 4 if gather else 1
    n = 1 + 2 + 2 + 6 + (0 if gather else 6) + 2 + 2 + 1
    return pl.pallas_call(
        functools.partial(reduce_kernel, rows, gather),
        out_shape=jax.ShapeDtypeStruct((slabs, rows, BLOCK), F32),
        in_specs=[pl.BlockSpec(memory_space=pltpu.VMEM)],
        out_specs=pl.BlockSpec(memory_space=pl.ANY),
        scratch_shapes=[
            pltpu.VMEM((rows // 2, BLOCK), F32),
            pltpu.VMEM((slabs, rows, BLOCK), F32),
            pltpu.VMEM((rows // 2, BLOCK), F32),
            pltpu.VMEM((rows // 8, BLOCK), F32),
            pltpu.VMEM((rows // 8, BLOCK), F32),
            pltpu.VMEM((rows // 16, BLOCK), F32),
            pltpu.VMEM((rows // 16, BLOCK), F32),
            pltpu.VMEM((6, 8 if gather else rows // 64, BLOCK), F32),
            pltpu.SemaphoreType.DMA((n,)),
            pltpu.SemaphoreType.DMA((n,)),
            pltpu.SemaphoreType.DMA,
        ],
        compiler_params=pltpu.CompilerParams(collective_id=ident, has_side_effects=True, vmem_limit_bytes=30 * 1024 * 1024),
        cost_estimate=pl.CostEstimate(flops=rows * 2000, bytes_accessed=100_000_000, transcendentals=0),
        name="reduce_gather" if gather else "reduce_all",
    )(part)


def lower_back(up, inv, x_ref, x0, base):
    for k in range(PAIR // PANEL - 1, -1, -1):
        a, b = k * PANEL, (k + 1) * PANEL
        v = base(a, b)
        if b < PAIR:
            v = v - jnp.sum(up[a:b, b:PAIR] * x_ref[0:1, x0 + b:x0 + PAIR], axis=1, keepdims=True)
        x_ref[0:1, x0 + a:x0 + b] = jnp.sum(inv[k] * v, axis=0, keepdims=True)


def load_half(planes, stage, sems, first, up, ridge):
    copies = [pltpu.make_async_copy(planes.at[first + i], stage.at[i], sems.at[i]) for i in range(2)]
    for copy in copies:
        copy.start()
    for copy in copies:
        copy.wait()
    diag = eye(BLOCK) * ridge
    for i in range(2):
        a, b = i * BLOCK, (i + 1) * BLOCK
        up[a:b, a:b] = stage[i, :BLOCK] + diag
        up[a:b, PAIR:] = stage[i, PAIR:].T
    up[:BLOCK, BLOCK:PAIR] = stage[0, BLOCK:PAIR] + stage[1, BLOCK:PAIR]


def low_kernel(planes, ridge, up, inv, stage, work, sems):
    load_half(planes, stage, sems, 0, up, ridge[0, 0])
    factor(up, inv, work, PAIR)


def high_kernel(planes, ridge, up_low, inv_low, cross, x_ref, stage, mid, up, inv, work, sems):
    load_half(planes, stage, sems, 2, up, ridge[0, 0])
    for i in range(2):
        for j in range(2):
            r = (2 * i + j) * BLOCK
            mid[i * BLOCK:(i + 1) * BLOCK, j * BLOCK:(j + 1) * BLOCK] = cross[0, r:r + BLOCK, :]
    mid[:, PAIR:] = up_low[:, PAIR:]
    panels = PAIR // PANEL
    for k in range(panels):
        a, b = k * PANEL, (k + 1) * PANEL
        mid[a:b, :PAIR] = dot(inv_low[k], mid[a:b, :PAIR])
        for i in range(k + 1, panels):
            c = i * PANEL
            mid[c:c + PANEL, :PAIR] = mid[c:c + PANEL, :PAIR] - dot(up_low[a:b, c:c + PANEL], mid[a:b, :PAIR], ((0,), (0,)))
    for i in range(panels):
        c = i * PANEL
        up[c:c + PANEL, c:] = up[c:c + PANEL, c:] - dot(mid[:, c:c + PANEL], mid[:, c:], ((0,), (0,)))
    factor(up, inv, work, PAIR)
    lower_back(up, inv, x_ref, PAIR, lambda a, b: up[a:b, PAIR:PAIR + 1])
    lower_back(up_low, inv_low, x_ref, 0, lambda a, b: up_low[a:b, PAIR:PAIR + 1] - jnp.sum(
        mid[a:b, :PAIR] * x_ref[0:1, PAIR:], axis=1, keepdims=True))


VM = pl.BlockSpec(memory_space=pltpu.VMEM)
SM = pl.BlockSpec(memory_space=pltpu.SMEM)
HB = pl.BlockSpec(memory_space=pl.ANY)
PANELS_SHAPE = (PAIR // PANEL, PANEL, PANEL)


def factor_low(planes, ridge):
    rows = planes.shape[1]
    return pl.pallas_call(
        low_kernel,
        out_shape=(jax.ShapeDtypeStruct((PAIR, PAIR + EXTRA), F32), jax.ShapeDtypeStruct(PANELS_SHAPE, F32)),
        in_specs=[HB, SM],
        out_specs=(VM, VM),
        scratch_shapes=[pltpu.VMEM((2, rows, BLOCK), F32), pltpu.VMEM((HALF, 2 * HALF), F32), pltpu.SemaphoreType.DMA((2,))],
        compiler_params=pltpu.CompilerParams(vmem_limit_bytes=24 * MIB),
        cost_estimate=pl.CostEstimate(flops=40_000_000_000, bytes_accessed=10_000_000, transcendentals=0),
        name="factor_low",
    )(planes, ridge)


def factor_high(planes, ridge, up_low, inv_low, cross):
    rows = planes.shape[1]
    return pl.pallas_call(
        high_kernel,
        out_shape=jax.ShapeDtypeStruct((1, 2 * PAIR), F32),
        in_specs=[HB, SM, VM, VM, VM],
        out_specs=VM,
        scratch_shapes=[
            pltpu.VMEM((2, rows, BLOCK), F32),
            pltpu.VMEM((PAIR, PAIR + EXTRA), F32),
            pltpu.VMEM((PAIR, PAIR + EXTRA), F32),
            pltpu.VMEM(PANELS_SHAPE, F32),
            pltpu.VMEM((HALF, 2 * HALF), F32),
            pltpu.SemaphoreType.DMA((2,)),
        ],
        compiler_params=pltpu.CompilerParams(vmem_limit_bytes=32 * MIB),
        cost_estimate=pl.CostEstimate(flops=50_000_000_000, bytes_accessed=10_000_000, transcendentals=0),
        name="factor_high",
    )(planes, ridge, up_low, inv_low, cross)


def cross_kernel(slot, steps, own, mate, far, prev, out, near, total):
    z = lax.axis_index('tp')
    i = pl.program_id(0)
    odd = lax.rem(z, 2)
    near[:, pl.ds(pl.multiple_of(odd * BLOCK, BLOCK), BLOCK)] = own[...]
    near[:, pl.ds(pl.multiple_of((1 - odd) * BLOCK, BLOCK), BLOCK)] = mate[...]

    @pl.when(i == 0)
    def _():
        total[...] = jnp.zeros_like(total)

    @pl.when(z < 2)
    def _():
        total[...] += dot(near[...], far[...], ((0,), (0,)))

    @pl.when(z >= 2)
    def _():
        total[:BLOCK] += dot(far[...], near[:, :BLOCK], ((0,), (0,)))
        total[BLOCK:] += dot(far[...], near[:, BLOCK:], ((0,), (0,)))

    def place(src, far_odd):
        for n in range(2):
            r = jnp.where(z < 2, 2 * n + far_odd, 2 * far_odd + n) * BLOCK
            out[pl.ds(pl.multiple_of(r, BLOCK), BLOCK), :] = src[n * BLOCK:(n + 1) * BLOCK, :]

    @pl.when(i == steps - 1)
    def _():
        if slot == 0:
            out[...] = total[...]
        else:
            place(prev, 1 - odd)
            place(total, odd)


def cross_gram(slot, design_blk, mate, far, prev, z_row):
    quarter = mate.shape[0]
    tile = 512
    steps = quarter // tile
    tile_spec = pl.BlockSpec((tile, BLOCK), lambda i, zr: (i, 0))
    whole = pl.BlockSpec(prev.shape, lambda i, zr: (0, 0))
    out_rows = PAIR if slot == 0 else 2 * PAIR
    return pl.pallas_call(
        lambda zr, *refs: cross_kernel(slot, steps, *refs),
        out_shape=jax.ShapeDtypeStruct((out_rows, BLOCK), F32),
        grid_spec=pltpu.PrefetchScalarGridSpec(
            num_scalar_prefetch=1,
            grid=(steps,),
            in_specs=[pl.BlockSpec((tile, BLOCK), lambda i, zr: (zr[0] * steps + i, 0)), tile_spec, tile_spec, whole],
            out_specs=pl.BlockSpec((out_rows, BLOCK), lambda i, zr: (0, 0)),
            scratch_shapes=[pltpu.VMEM((tile, PAIR), F32), pltpu.VMEM((PAIR, BLOCK), F32)],
        ),
        compiler_params=pltpu.CompilerParams(dimension_semantics=("arbitrary",), vmem_limit_bytes=30 * MIB),
        cost_estimate=pl.CostEstimate(flops=8_000_000_000, bytes_accessed=12_000_000, transcendentals=0),
    )(z_row, design_blk, mate, far, prev)


def residual_kernel(steps, design, x_ref, target, out, fits, send_sem, recv_sem):
    z, dp = lax.axis_index('tp'), lax.axis_index('dp')
    i = pl.program_id(0)
    tile = design.shape[0]
    peers = [{'tp': p, 'dp': dp} for p in z_peers(z)]

    @pl.when(i == 0)
    def _():
        barrier = pltpu.get_barrier_semaphore()
        for peer in peers:
            pl.semaphore_signal(barrier, inc=1, device_id=peer, device_id_type=MESH)
        pl.semaphore_wait(barrier, 3)

    x = [x_ref[0:1, pl.ds(pl.multiple_of(z * BLOCK + c * HALF, HALF), HALF)] for c in range(BLOCK // HALF)]
    rows = []
    for r in range(tile // HALF):
        t = sum(design[r * HALF:(r + 1) * HALF, c * HALF:(c + 1) * HALF] * x[c] for c in range(BLOCK // HALF))
        rows.append(jnp.sum(t.T, axis=0, keepdims=True))
    per = tile // HALF
    fits[0, pl.ds(pl.multiple_of(i * per, per), per), :] = jnp.concatenate(rows, axis=0)

    @pl.when(i == steps - 1)
    def _():
        copies = []
        for j, peer in enumerate(peers):
            copy = pltpu.make_async_remote_copy(src_ref=fits.at[0], dst_ref=fits.at[j + 1], send_sem=send_sem.at[j], recv_sem=recv_sem.at[j], device_id=peer, device_id_type=MESH)
            copy.start()
            copies.append(copy)
        for copy in copies:
            copy.wait()
        lo = jnp.where(z % 2 == 0, fits[0] + fits[1], fits[1] + fits[0])
        hi = jnp.where(z % 2 == 0, fits[2] + fits[3], fits[3] + fits[2])
        out[...] = target[...] - (lo + hi)


def residual(design_blk, x_row, target_tile):
    rows = design_blk.shape[0]
    tile = 1024
    steps = rows // tile
    whole = pl.BlockSpec(target_tile.shape, lambda i: (0, 0))
    return pl.pallas_call(
        functools.partial(residual_kernel, steps),
        out_shape=jax.ShapeDtypeStruct(target_tile.shape, F32),
        grid=(steps,),
        in_specs=[pl.BlockSpec((tile, BLOCK), lambda i: (i, 0)), pl.BlockSpec(x_row.shape, lambda i: (0, 0)), whole],
        out_specs=whole,
        scratch_shapes=[pltpu.VMEM((4,) + target_tile.shape, F32), pltpu.SemaphoreType.DMA((3,)), pltpu.SemaphoreType.DMA((3,))],
        compiler_params=pltpu.CompilerParams(collective_id=3, has_side_effects=True, dimension_semantics=("arbitrary",), vmem_limit_bytes=24 * MIB),
        cost_estimate=pl.CostEstimate(flops=6_000_000_000, bytes_accessed=13_000_000, transcendentals=0),
        name="residual",
    )(design_blk, x_row, target_tile)


def solution(mesh):
    col_ways, row_ways = mesh.shape['tp'], mesh.shape['dp']

    def swap(block, mask):
        pairs = [(t * row_ways + d, (t ^ mask) * row_ways + d) for t in range(col_ways) for d in range(row_ways)]
        return lax.ppermute(block, ('tp', 'dp'), pairs)

    def local_fit(design_blk, target_blk, ridge):
        rows_dev, _ = design_blk.shape
        quarter_rows = rows_dev // col_ways
        z = lax.axis_index('tp')

        def quarter(index):
            return lax.dynamic_slice_in_dim(design_blk, index * quarter_rows, quarter_rows)

        mate_a = swap(quarter(z ^ 1), 1)
        mate_b = swap(quarter(z ^ 3), 1)
        far_c = swap(quarter(z ^ 3), 3)
        far_d = swap(quarter(z ^ 2), 2)
        own_gram = dot(design_blk, design_blk, ((0,), (0,)))
        moment = dot(target_blk[None, :], design_blk)
        pair_gram = dot(quarter(z), mate_a, ((0,), (0,))) + dot(quarter(z ^ 2), mate_b, ((0,), (0,)))
        pair_gram = jnp.where(z % 2 == 0, pair_gram, pair_gram.T)
        part = jnp.concatenate([own_gram, pair_gram, jnp.pad(moment, ((0, EXTRA - 1), (0, 0)))], axis=0)
        planes = reduce_all(part, True, 1)
        ridge_cell = jnp.reshape(ridge, (1, 1))
        up_low, inv_low = factor_low(planes, ridge_cell)
        z_row = jnp.reshape(z, (1,)).astype(jnp.int32)
        first = cross_gram(0, design_blk, mate_a, far_c, jnp.zeros((8, HALF), F32), z_row)
        cross = cross_gram(1, design_blk, mate_a, far_d, first, z_row)
        cross = reduce_all(cross, False, 2)
        x_row = factor_high(planes, ridge_cell, up_low, inv_low, cross)
        left = residual(design_blk, x_row, jnp.reshape(target_blk, (rows_dev // HALF, HALF)))
        return x_row[0], jnp.reshape(left, (rows_dev,))

    return jax.shard_map(local_fit, mesh=mesh, in_specs=(P('dp', 'tp'), P('dp'), P()), out_specs=(P(), P('dp')), check_vma=False)
```

time: 713 us -> 532 us (0.75)
  waiting for transfers between devices: 473 us -> 225 us
  Pallas kernels: 85.6 us -> 222 us
  matrix products: 92.5 us -> 48.1 us
  blocking collectives: 18.1 us -> 0 us
  between operations: 14.7 us -> 1.92 us
  other arithmetic: 9.62 us -> 0.77 us
  local copies, waits for them, and re-layouts: 12.6 us -> 20.7 us
    all_to_all x1 -> x0, waiting for transfers between devices: 274 us -> none  [local_fit(): row_panel = lax.all_to_all(design_blk, 'tp', 0, 1, tiled=True)]
    ppermute x0 -> x4, waiting for transfers between devices: none -> 225 us  [swap(): return lax.ppermute(block, ('tp', 'dp'), pairs)]
    psum x1 -> x0, waiting for transfers between devices: 198 us -> none  [local_fit(): gram_aug = lax.psum(gram_part, ('tp', 'dp'))]
    pallas_call x1 -> x7, Pallas kernels: 85.6 us -> 222 us  [the longest x2 102 us: reduce_all(): pl.pallas_call(functools.partial(reduce_kernel, rows, gather), out_shape=...]
    dot_general x2 -> x4, matrix products: 92.5 us -> 48.1 us  [dot(): lax.dot_general(a, b, (dims, ((), ())), precision=HIGHEST, preferred_elem...]
    psum x1 -> x0, blocking collectives: 18.1 us -> none  [local_fit(): fitted = lax.psum(dot(design_blk, coeff_blk, ((1,), (0,))), 'tp')]
    all_to_all x1 -> x0, local copies, waits for them, and re-layouts: 12.6 us -> none  [local_fit(): row_panel = lax.all_to_all(design_blk, 'tp', 0, 1, tiled=True)]
    unnamed x2 -> x15, local copies, waits for them, and re-layouts: 0.01 us -> 9.79 us
  transfers between devices with their start and end apart: 2 -> 4, of which waited for: 2 -> 2; matrix products, arithmetic and copies ran while one was open for 0% -> 10% of each run, Pallas kernels for 0% -> 2%
where the time goes in v2:
time: 532 us; the launch traced here: 526 us
  waiting for transfers between devices  225 us (42%)
  Pallas kernels  222 us (42%)
  matrix products  48.1 us (9%)
  local copies, waits for them, and re-layouts  20.7 us (4%)
  starting transfers between devices  7.11 us (1%)
    ppermute x4, waiting for transfers between devices, swap(): return lax.ppermute(block, ('tp', 'dp'), pairs)  225 us
    pallas_call x2, Pallas kernels, reduce_all(): pl.pallas_call(functools.partial(reduce_kernel, rows, gather), out_shape=...  102 us
    pallas_call x1, Pallas kernels, factor_high(): pl.pallas_call(high_kernel, out_shape=jax.ShapeDtypeStruct((1, 2 * PAIR),...  48.2 us
    dot_general x4, matrix products, dot(): lax.dot_general(a, b, (dims, ((), ())), precision=HIGHEST, preferred_elem...  48.1 us
    pallas_call x1, Pallas kernels, factor_low(): pl.pallas_call(low_kernel, out_shape=(jax.ShapeDtypeStruct((PAIR, PAIR +...  36.1 us
    pallas_call x2, Pallas kernels, cross_gram(): pl.pallas_call(lambda zr, *refs: cross_kernel(slot, steps, *refs), out_sh...  25.8 us
  transfers between devices with their start and end apart: 4, of which 2 were waited for; matrix products, arithmetic and copies ran while one was open for 10% of the time, Pallas kernels for 2%

profile of v2, /device:TPU:0, one launch (start us, length us, event | category | flops | bytes accessed | tf_op | source)
XLA Modules:
  0.0 526.0 jit_solution(12383868736282172530)
XLA Ops:
  0.7 8.8 %constant_dynamic-slice_fusion.2 = (f32[2048,384]{1,0:T(8,128)}, f32[2048,384]{1,0:T(8,128)}, f32[2048,384]{1,0:T(8,128)}) fusion(f32[8192,384]{1,0:T(8,128)} %design.1, s32[]{:T(128)S(6)} %select_n.32, s32[]{:T(128)S(6)} %select_n.34, s32[]{:T(128)S(6)} %select_n.33), kind=kLoop, calls=%fused_computation.8 | loop fusion | bytes 18874380 | tf_op jit(solution)/shard_map/dynamic_slice | solution.py:414
  9.5 3.1 collective-permute-start.1
  12.5 0.0 collective-permute-start
  12.6 4.0 collective-permute-start.3
  16.6 6.1 %fusion.8 = f32[1,384]{1,0:T(1,128)S(1)} fusion(f32[8192,1]{0,1:T(1,128)S(1)} %bitcast.16, f32[8192,384]{1,0:T(8,128)S(1)} %copy-done), kind=kOutput, calls=%fused_computation.12 | convolution fusion | flops 37748736 | bytes 12617216 | tf_op jit(solution)/shard_map/dot_general | solution.py:18
  23.3 26.3 %fusion.6 = f32[384,384]{1,0:T(8,128)} fusion(f32[8192,384]{1,0:T(8,128)} %design.1), kind=kOutput, calls=%fused_computation.10 | convolution fusion | flops 14495514624 | bytes 13172736 | tf_op jit(solution)/shard_map/dot_general | solution.py:18
  49.6 32.2 %collective-permute-done.1 = f32[2048,384]{1,0:T(8,128)} collective-permute-done((f32[2048,384]{1,0:T(8,128)}, f32[2048,384]{1,0:T(8,128)}, u32[]{:S(2)}, u32[]{:S(2)}) %collective-permute-start.1) | collective-permute-done | bytes 3145760 | tf_op jit(solution)/shard_map/ppermute | solution.py:406
  81.8 7.9 %fusion.7 = f32[384,384]{0,1:T(8,128)S(1)} fusion(f32[2048,384]{1,0:T(8,128)} %get-tuple-element.8, f32[2048,384]{1,0:T(8,128)} %collective-permute-done.1), kind=kOutput, calls=%fused_computation.11 | convolution fusion | flops 3623878656 | bytes 6881280 | tf_op jit(solution)/shard_map/dot_general | solution.py:18
  89.7 192.9 %collective-permute-done.refs_1_ = f32[2048,384]{1,0:T(8,128)S(1)} collective-permute-done((f32[2048,384]{1,0:T(8,128)}, f32[2048,384]{1,0:T(8,128)S(1)}, u32[]{:S(2)}, u32[]{:S(2)}) %collective-permute-start) | collective-permute-done | bytes 3145760 | tf_op jit(solution)/shard_map/ppermute | solution.py:406
  282.7 7.8 %fusion.2 = f32[384,384]{0,1:T(8,128)} fusion(f32[384,384]{0,1:T(8,128)S(1)} %fusion.7, f32[2048,384]{1,0:T(8,128)S(1)} %collective-permute-done.refs_1_, f32[8192,384]{1,0:T(8,128)} %design.1, s32[]{:T(128)S(6)} %select_n.31), kind=kOutput, calls=%fused_computation.4 | convolution fusion | flops 3624026112 | bytes 7471108 | tf_op jit(solution)/shard_map/dot_general | solution.py:18
  290.5 2.1 copy.7
  292.6 4.6 copy-done.1
  297.2 13.1 %shard_map.50.refs_3_ = f32[768,384]{1,0:T(8,128)S(1)} custom-call(s32[1]{0:T(128)} %bitcast.3.zr, f32[8192,384]{1,0:T(8,128)S(1)} %copy-done.1, f32[2048,384]{1,0:T(8,128)S(1)} %collective-permute-done.refs_1_, f32[2048,384]{1,0:T(8,128)} %collective-permute-done.3.refs_2_, f32[8,128]{1,0:T(8,128)S(1)} %broadcast_in_dim.4.refs_3_), custom_call_target="tpu_custom_call" | custom-call | flops 8000000000 | bytes 12000000 | tf_op jit(solution)/shard_map/pallas_call | solution.py:333
  310.3 12.7 %shard_map.51.part = f32[1536,384]{1,0:T(8,128)S(1)} custom-call(s32[1]{0:T(128)} %bitcast.3.zr, f32[8192,384]{1,0:T(8,128)S(1)} %copy-done.1, f32[2048,384]{1,0:T(8,128)S(1)} %collective-permute-done.refs_1_, f32[2048,384]{1,0:T(8,128)} %collective-permute-done.2.refs_2_, f32[768,384]{1,0:T(8,128)S(1)} %shard_map.50.refs_3_), custom_call_target="tpu_custom_call" | custom-call | flops 8000000000 | bytes 12000000 | tf_op jit(solution)/shard_map/pallas_call | solution.py:333
  323.1 47.7 %reduce_all.1.cross = f32[1,1536,384]{2,1,0:T(8,128)S(1)} custom-call(f32[1536,384]{1,0:T(8,128)S(1)} %shard_map.51.part), custom_call_target="tpu_custom_call" | custom-call | flops 3072000 | bytes 100000000 | tf_op jit(solution)/shard_map/reduce_all/pallas_call | solution.py:176
  370.8 0.1 bitcast_select_fusion
  370.9 0.1 select_maximum_fusion.part
  371.0 54.3 %reduce_gather.1.planes = f32[4,896,384]{2,1,0:T(8,128)S(1)} custom-call(f32[896,384]{1,0:T(8,128)S(1)} %select_maximum_fusion.part), custom_call_target="tpu_custom_call" | custom-call | flops 1792000 | bytes 100000000 | tf_op jit(solution)/shard_map/reduce_gather/pallas_call | solution.py:176
  425.3 36.1 %factor_low.1 = (f32[768,896]{1,0:T(8,128)S(1)}, f32[3,256,256]{2,1,0:T(8,128)S(1)}) custom-call(f32[4,896,384]{2,1,0:T(8,128)S(1)} %reduce_gather.1.planes, f32[1,1]{1,0:T(1,128)} %bitcast.14.ridge), custom_call_target="tpu_custom_call" | custom-call | flops 40000000000 | bytes 10000000 | tf_op jit(solution)/shard_map/factor_low/pallas_call | solution.py:259
  461.4 48.2 %factor_high.1.x_ref = f32[1,1536]{1,0:T(1,128)S(1)} custom-call(f32[4,896,384]{2,1,0:T(8,128)S(1)} %reduce_gather.1.planes, f32[1,1]{1,0:T(1,128)} %bitcast.15.ridge, f32[768,896]{1,0:T(8,128)S(1)} %get-tuple-element.4.up_low, f32[3,256,256]{2,1,0:T(8,128)S(1)} %get-tuple-element.5.inv_low, f32[1,1536,384]{2,1,0:T(8,128)S(1)} %reduce_all.1.cross), custom_call_target="tpu_custom_call" | custom-call | flops 49999998976 | bytes 10000000 | tf_op jit(solution)/shard_map/factor_high/pallas_call | solution.py:273
  509.5 0.6 reduce
  510.2 4.6 copy-done.2
  514.7 10.1 %residual.1 = f32[64,128]{1,0:T(8,128)S(1)} custom-call(f32[8192,384]{1,0:T(8,128)S(1)} %copy-done.2, f32[1,1536]{1,0:T(1,128)S(1)} %factor_high.1.x_ref, f32[64,128]{1,0:T(8,128)S(1)} %bitcast.17), custom_call_target="tpu_custom_call" | custom-call | flops 6000000000 | bytes 13000000 | tf_op jit(solution)/shard_map/residual/pallas_call | solution.py:388
  524.9 0.6 copy.12
  (16 shorter events, 0.0 us)
Async XLA Ops:
  0.7 15.9 %copy-start = (f32[8192,384]{1,0:T(8,128)S(1)}, f32[8192,384]{1,0:T(8,128)}, u32[]{:S(2)}) copy-start(f32[8192,384]{1,0:T(8,128)} %design.1) | copy-start | bytes 37748740
  0.7 15.9 %copy-start.3 = (f32[8192]{0:T(1024)S(1)}, f32[8192]{0:T(1024)}, u32[]{:S(2)}) copy-start(f32[8192]{0:T(1024)} %param.4) | copy-start | bytes 98308
  9.5 72.3 %collective-permute-start.1 = (f32[2048,384]{1,0:T(8,128)}, f32[2048,384]{1,0:T(8,128)}, u32[]{:S(2)}, u32[]{:S(2)}) collective-permute-start(f32[2048,384]{1,0:T(8,128)} %get-tuple-element.7), channel_id=1, source_target_pairs={{0,8},{1,9},{2,10},{3,11},{4,12},{5,13},{6,14},{7,15},{8,0},{9,1},... | collective-permute-start | bytes 9437192 | tf_op jit(solution)/shard_map/ppermute | solution.py:406
  12.5 270.1 %collective-permute-start = (f32[2048,384]{1,0:T(8,128)}, f32[2048,384]{1,0:T(8,128)S(1)}, u32[]{:S(2)}, u32[]{:S(2)}) collective-permute-start(f32[2048,384]{1,0:T(8,128)} %get-tuple-element.6), channel_id=1, source_target_pairs={{0,8},{1,9},{2,10},{3,11},{4,12},{5,13},{6,14},{7,15},{8,0},{9,1},... | collective-permute-start | bytes 9437192 | tf_op jit(solution)/shard_map/ppermute | solution.py:406
  12.6 280.1 %collective-permute-start.3 = (f32[2048,384]{1,0:T(8,128)}, f32[2048,384]{1,0:T(8,128)}, u32[]{:S(2)}, u32[]{:S(2)}) collective-permute-start(f32[2048,384]{1,0:T(8,128)} %get-tuple-element.7), channel_id=1, source_target_pairs={{0,24},{1,25},{2,26},{3,27},{4,28},{5,29},{6,30},{7,31},{8,16},{9,... | collective-permute-start | bytes 9437192 | tf_op jit(solution)/shard_map/ppermute | solution.py:406
  16.6 293.7 %collective-permute-start.2 = (f32[2048,384]{1,0:T(8,128)}, f32[2048,384]{1,0:T(8,128)}, u32[]{:S(2)}, u32[]{:S(2)}) collective-permute-start(f32[2048,384]{1,0:T(8,128)} %get-tuple-element.8), channel_id=1, source_target_pairs={{0,16},{1,17},{2,18},{3,19},{4,20},{5,21},{6,22},{7,23},{8,24},{9,... | collective-permute-start | bytes 9437192 | tf_op jit(solution)/shard_map/ppermute | solution.py:406
  292.6 4.6 copy-start.1
  323.0 47.8 %copy-start.4 = (f32[384,384]{0,1:T(8,128)S(1)}, f32[384,384]{0,1:T(8,128)}, u32[]{:S(2)}) copy-start(f32[384,384]{0,1:T(8,128)} %fusion.2) | copy-start | bytes 1769476
  323.0 47.8 %copy-start.5 = (f32[384,384]{1,0:T(8,128)S(1)}, f32[384,384]{1,0:T(8,128)}, u32[]{:S(2)}) copy-start(f32[384,384]{1,0:T(8,128)} %copy.7) | copy-start | bytes 1769476
  323.1 47.8 %copy-start.6 = (f32[384,384]{1,0:T(8,128)S(1)}, f32[384,384]{1,0:T(8,128)}, u32[]{:S(2)}) copy-start(f32[384,384]{1,0:T(8,128)} %fusion.6) | copy-start | bytes 1769476
  510.2 4.6 copy-start.2

commit v3 on v2

v3 whole, which is shorter than its diff:
```python
import functools
import jax
import jax.numpy as jnp
from jax import lax
from jax.experimental import pallas as pl
from jax.experimental.pallas import tpu as pltpu
from jax.sharding import PartitionSpec as P

HIGHEST = lax.Precision.HIGHEST
F32 = jnp.float32
SUB, HALF, PANEL, BLOCK, EXTRA = 16, 128, 256, 384, 128
PAIR = 2 * BLOCK
MESH = pl.DeviceIdType.MESH
MIB = 1024 * 1024


def dot(a, b, dims=((1,), (0,))):
    return lax.dot_general(a, b, (dims, ((), ())), precision=HIGHEST, preferred_element_type=F32)


def micro_rows(left, right, col0):
    rows = lax.broadcasted_iota(jnp.int32, (SUB, HALF), 0)
    cols = [jnp.broadcast_to(left[:, col0 + c:col0 + c + 1], (SUB, HALF)) for c in range(SUB)]
    pivots = cols[0]
    for p in range(SUB):
        inv = 1.0 / cols[p][p:p + 1, :]
        fac = jnp.where(rows > p, cols[p] * inv, 0.0)
        for c in range(p + 1, SUB):
            cols[c] = cols[c] - fac * cols[c][p:p + 1, :]
        left = left - fac * left[p:p + 1, :]
        right = right - fac * right[p:p + 1, :]
        pivots = jnp.where(rows == p, cols[p], pivots)
    scale = lax.rsqrt(pivots)
    return left * scale, right * scale


def invert_factor(work, inv_ref):
    for m in range(HALF // SUB):
        r = m * SUB
        left, right = micro_rows(work[r:r + SUB, :HALF], work[r:r + SUB, HALF:], r)
        inv_ref[r:r + SUB, :] = right
        if r + SUB < HALF:
            both = jnp.concatenate([left, right], axis=1)
            upd = dot(left, both, ((0,), (0,)))
            work[r + SUB:, :] = work[r + SUB:, :] - upd[r + SUB:, :]


def eye(n):
    rows = lax.broadcasted_iota(jnp.int32, (n, n), 0)
    return jnp.where(rows == lax.broadcasted_iota(jnp.int32, (n, n), 1), 1.0, 0.0).astype(F32)


def factor(up, inv, work, small, n):
    panels = n // PANEL
    first, carry = small.at[0], small.at[1]

    def step(t, _):
        k, odd = t // 2, lax.rem(t, 2)
        r0 = pl.multiple_of(t * HALF, HALF)
        r1 = pl.multiple_of(t * HALF + HALF * (1 - odd), HALF)
        work[:, :HALF] = up[pl.ds(r0, HALF), pl.ds(r0, HALF)]
        work[:, HALF:] = eye(HALF)
        invert_factor(work, first)

        @pl.when(odd == 0)
        def _():
            w1 = first[...]
            inv[k] = jnp.zeros((PANEL, PANEL), F32)
            inv[k, :HALF, :HALF] = w1
            u12 = dot(w1, up[pl.ds(r0, HALF), pl.ds(r1, HALF)])
            both = dot(u12, jnp.concatenate([u12, w1], axis=1), ((0,), (0,)))
            up[pl.ds(r1, HALF), pl.ds(r1, HALF)] = up[pl.ds(r1, HALF), pl.ds(r1, HALF)] - both[:, :HALF]
            carry[...] = both[:, HALF:]

        @pl.when(odd == 1)
        def _():
            w2 = first[...]
            inv[k, HALF:, HALF:] = w2
            inv[k, HALF:, :HALF] = -dot(w2, carry[...])

        for kk in range(panels):
            @pl.when(t == 2 * kk + 1)
            def _():
                a, b = kk * PANEL, (kk + 1) * PANEL
                up[a:b, b:] = dot(inv[kk], up[a:b, b:])
                for i in range(kk + 1, panels):
                    c = i * PANEL
                    up[c:c + PANEL, c:] = up[c:c + PANEL, c:] - dot(up[a:b, c:c + PANEL], up[a:b, c:], ((0,), (0,)))
        return 0

    lax.fori_loop(0, 2 * panels, step, 0)


def places():
    z, dp = lax.axis_index('tp'), lax.axis_index('dp')
    core, x, y = lax.rem(dp, 2), lax.rem(dp // 2, 2), dp // 4
    return z, dp, core, x, y


def z_peers(z):
    return (z + 1 - 2 * lax.rem(z, 2), z + 2 - 4 * (z // 2), 3 - z)


def plane_peers(z, dp, core, x, y):
    return ({'tp': z, 'dp': dp + 1 - 2 * core}, {'tp': z, 'dp': dp + 2 - 4 * x}, {'tp': z, 'dp': dp + 4 - 8 * y})


def meet(peers):
    barrier = pltpu.get_barrier_semaphore()
    for peer in peers:
        pl.semaphore_signal(barrier, inc=1, device_id=peer, device_id_type=MESH)
    pl.semaphore_wait(barrier, len(peers))


def starter(send_sem, recv_sem):
    count = [0]

    def start(src, dst, peer):
        i = count[0]
        count[0] += 1
        copy = pltpu.make_async_remote_copy(src_ref=src, dst_ref=dst, send_sem=send_sem.at[i], recv_sem=recv_sem.at[i], device_id=peer, device_id_type=MESH)
        copy.start()
        return copy

    return start


def at(base, size):
    return pl.ds(pl.multiple_of(base, 8), size)


def spans(rows, core, x, y):
    half, quart, eighth, sixt = rows // 2, rows // 4, rows // 8, rows // 16
    a1, b1 = x * eighth, quart + y * eighth
    return core * half, a1, b1, a1 + y * sixt, b1 + x * sixt


def plane_scatter(rows, part, acc, got, start, peers, where):
    _, _, core, x, y = where
    core_peer, x_peer, y_peer = peers
    half, quart, eighth, sixt = rows // 2, rows // 4, rows // 8, rows // 16
    own, a1, b1, a2, b2 = spans(rows, core, x, y)
    got_core, got_a, got_b, got_a2, got_b2 = got
    copy = start(part.at[at((1 - core) * half, half)], got_core, core_peer)
    yield
    copy.wait()
    acc[...] = part[at(own, half)] + got_core[...]
    copies = [start(acc.at[at((1 - x) * eighth, eighth)], got_a, x_peer), start(acc.at[at(quart + (1 - y) * eighth, eighth)], got_b, y_peer)]
    yield
    copies[0].wait()
    acc[at(a1, eighth)] = acc[at(a1, eighth)] + got_a[...]
    copies[1].wait()
    acc[at(b1, eighth)] = acc[at(b1, eighth)] + got_b[...]
    copies = [start(acc.at[at(a1 + (1 - y) * sixt, sixt)], got_a2, y_peer), start(acc.at[at(b1 + (1 - x) * sixt, sixt)], got_b2, x_peer)]
    yield
    copies[0].wait()
    acc[at(a2, sixt)] = acc[at(a2, sixt)] + got_a2[...]
    copies[1].wait()
    acc[at(b2, sixt)] = acc[at(b2, sixt)] + got_b2[...]


def plane_gather(rows, full, start, peers, where):
    _, _, core, x, y = where
    core_peer, x_peer, y_peer = peers
    half, eighth, sixt = rows // 2, rows // 8, rows // 16
    own, a1, b1, a2, b2 = spans(rows, core, x, y)
    for sizes in (((a2, sixt, y_peer), (b2, sixt, x_peer)), ((a1, eighth, x_peer), (b1, eighth, y_peer)), ((0, half, core_peer),)):
        copies = []
        for base, size, peer in sizes:
            ref = full.at[:, at(own + base, size)]
            copies.append(start(ref, ref, peer))
        yield
        for copy in copies:
            copy.wait()


def in_turn(chunks):
    chunks = list(chunks)
    while chunks:
        chunks = [chunk for chunk in chunks if next(chunk, chunks) is not chunks]


def wait_all(copies):
    for copy in copies:
        copy.wait()


def sum_chunk(rows, part, acc, full, got, got_z, start, peers, z_peer, where):
    z, _, core, x, y = where
    yield from plane_scatter(rows, part, acc, got, start, peers, where)
    own, _, _, a2, b2 = spans(rows, core, x, y)
    share = rows // 64
    copies = []
    for k, piece in enumerate((a2, b2)):
        for j, peer in enumerate(z_peer):
            copies.append(start(acc.at[at(piece + peer['tp'] * share, share)], got_z.at[2 * j + k], peer))
    yield
    wait_all(copies)
    copies = []
    for k, piece in enumerate((a2, b2)):
        mine = piece + z * share
        full[0, at(own + mine, share)] = (acc[at(mine, share)] + got_z[k]) + (got_z[2 + k] + got_z[4 + k])
        ref = full.at[0, at(own + mine, share)]
        copies += [start(ref, ref, peer) for peer in z_peer]
    yield
    wait_all(copies)
    yield from plane_gather(rows, full, start, peers, where)


CHUNKS = 2


def sum_kernel(rows, part, out, acc, full, g0, g1, g2, g3, g4, got_z, send_sem, recv_sem, out_sem):
    where = places()
    z, dp = where[:2]
    peers = plane_peers(*where)
    z_peer = [{'tp': p, 'dp': dp} for p in z_peers(z)]
    meet(list(peers) + z_peer)
    start = starter(send_sem, recv_sem)
    size = rows // CHUNKS
    in_turn(sum_chunk(size, part.at[c * size:(c + 1) * size], acc.at[c], full.at[:, c * size:(c + 1) * size],
                      [g.at[c] for g in (g0, g1, g2, g3, g4)], got_z.at[c], start, peers, z_peer, where) for c in range(CHUNKS))
    copy = pltpu.make_async_copy(full, out, out_sem)
    copy.start()
    copy.wait()


def stack_kernel(rows, part, out, acc, mine, g0, g1, g2, g3, g4, send_sem, recv_sem, out_sem):
    where = places()
    z, dp, core, x, y = where
    peers = plane_peers(*where)
    z_peer = [{'tp': p, 'dp': dp} for p in z_peers(z)]
    meet(list(peers) + z_peer)
    start = starter(send_sem, recv_sem)
    in_turn([plane_scatter(rows, part, acc.at[0], [g.at[0] for g in (g0, g1, g2, g3, g4)], start, peers, where)])
    _, _, _, a2, b2 = spans(rows, core, x, y)
    sixt = rows // 16
    mine[z, :sixt] = acc[0, at(a2, sixt)]
    mine[z, sixt:] = acc[0, at(b2, sixt)]
    wait_all([start(mine.at[z], mine.at[z], peer) for peer in z_peer])
    copy = pltpu.make_async_copy(mine, out, out_sem)
    copy.start()
    copy.wait()


def spread_kernel(rows, mine, out, full, send_sem, recv_sem, out_sem):
    where = places()
    _, _, core, x, y = where
    peers = plane_peers(*where)
    meet(peers)
    own, _, _, a2, b2 = spans(rows, core, x, y)
    sixt = rows // 16
    full[:, at(own + a2, sixt)] = mine[:, :sixt]
    full[:, at(own + b2, sixt)] = mine[:, sixt:]
    start = starter(send_sem, recv_sem)
    in_turn(plane_gather(rows, full.at[2 * c:2 * c + 2], start, peers, where) for c in range(2))
    copy = pltpu.make_async_copy(full, out, out_sem)
    copy.start()
    copy.wait()


def scatter_scratch(chunks, rows):
    return [pltpu.VMEM((chunks, rows // d, BLOCK), F32) for d in (2, 8, 8, 16, 16)]


def comm_call(body, rows, operand, out_shape, scratch, copies, ident):
    return pl.pallas_call(
        functools.partial(body, rows),
        out_shape=jax.ShapeDtypeStruct(out_shape, F32),
        in_specs=[pl.BlockSpec(memory_space=pltpu.VMEM)],
        out_specs=pl.BlockSpec(memory_space=pl.ANY),
        scratch_shapes=scratch + [pltpu.SemaphoreType.DMA((copies,)), pltpu.SemaphoreType.DMA((copies,)), pltpu.SemaphoreType.DMA],
        compiler_params=pltpu.CompilerParams(collective_id=ident, has_side_effects=True, vmem_limit_bytes=24 * MIB),
        cost_estimate=pl.CostEstimate(flops=rows * 2000, bytes_accessed=80_000_000, transcendentals=0),
    )(operand)


def sum_all(part, ident):
    rows = part.shape[0]
    size = rows // CHUNKS
    scratch = [pltpu.VMEM((CHUNKS, size // 2, BLOCK), F32), pltpu.VMEM((1, rows, BLOCK), F32)] + scatter_scratch(CHUNKS, size) + [pltpu.VMEM((CHUNKS, 6, size // 64, BLOCK), F32)]
    return comm_call(sum_kernel, rows, part, (1, rows, BLOCK), scratch, 22 * CHUNKS, ident)


def stack_planes(part, ident):
    rows = part.shape[0]
    scratch = [pltpu.VMEM((1, rows // 2, BLOCK), F32), pltpu.VMEM((4, rows // 8, BLOCK), F32)] + scatter_scratch(1, rows)
    return comm_call(stack_kernel, rows, part, (4, rows // 8, BLOCK), scratch, 8, ident)


def spread_planes(mine, ident):
    rows = mine.shape[1] * 8
    return comm_call(spread_kernel, rows, mine, (4, rows, BLOCK), [pltpu.VMEM((4, rows, BLOCK), F32)], 10, ident)


def lower_back(up, inv, x_ref, x0, base):
    for k in range(PAIR // PANEL - 1, -1, -1):
        a, b = k * PANEL, (k + 1) * PANEL
        v = base(a, b)
        if b < PAIR:
            v = v - jnp.sum(up[a:b, b:PAIR] * x_ref[0:1, x0 + b:x0 + PAIR], axis=1, keepdims=True)
        x_ref[0:1, x0 + a:x0 + b] = jnp.sum(inv[k] * v, axis=0, keepdims=True)


def load_half(planes, stage, sems, first, up, ridge):
    copies = [pltpu.make_async_copy(planes.at[first + i], stage.at[i], sems.at[i]) for i in range(2)]
    for copy in copies:
        copy.start()
    for copy in copies:
        copy.wait()
    diag = eye(BLOCK) * ridge
    for i in range(2):
        a, b = i * BLOCK, (i + 1) * BLOCK
        up[a:b, a:b] = stage[i, :BLOCK] + diag
        up[a:b, PAIR:] = stage[i, PAIR:].T


def low_kernel(planes, ridge, up, inv, stage, work, small, sems):
    load_half(planes, stage, sems, 0, up, ridge[0, 0])
    up[:BLOCK, BLOCK:PAIR] = stage[0, BLOCK:PAIR] + stage[1, BLOCK:PAIR]
    factor(up, inv, work, small, PAIR)


def high_kernel(planes, ridge, up_low, inv_low, cross, x_ref, stage, mid, up, inv, work, small, sems):
    load_half(planes, stage, sems, 2, up, ridge[0, 0])
    up[:BLOCK, BLOCK:PAIR] = cross[0, 2 * PAIR:2 * PAIR + BLOCK]
    for j in range(2):
        mid[:, j * BLOCK:(j + 1) * BLOCK] = cross[0, j * PAIR:(j + 1) * PAIR, :]
    mid[:, PAIR:] = up_low[:, PAIR:]
    panels = PAIR // PANEL
    for k in range(panels):
        a, b = k * PANEL, (k + 1) * PANEL
        mid[a:b, :PAIR] = dot(inv_low[k], mid[a:b, :PAIR])
        for i in range(k + 1, panels):
            c = i * PANEL
            mid[c:c + PANEL, :PAIR] = mid[c:c + PANEL, :PAIR] - dot(up_low[a:b, c:c + PANEL], mid[a:b, :PAIR], ((0,), (0,)))
    for i in range(panels):
        c = i * PANEL
        up[c:c + PANEL, c:] = up[c:c + PANEL, c:] - dot(mid[:, c:c + PANEL], mid[:, c:], ((0,), (0,)))
    factor(up, inv, work, small, PAIR)
    lower_back(up, inv, x_ref, PAIR, lambda a, b: up[a:b, PAIR:PAIR + 1])
    lower_back(up_low, inv_low, x_ref, 0, lambda a, b: up_low[a:b, PAIR:PAIR + 1] - jnp.sum(
        mid[a:b, :PAIR] * x_ref[0:1, PAIR:], axis=1, keepdims=True))


VM = pl.BlockSpec(memory_space=pltpu.VMEM)
SM = pl.BlockSpec(memory_space=pltpu.SMEM)
HB = pl.BlockSpec(memory_space=pl.ANY)
PANELS_SHAPE = (PAIR // PANEL, PANEL, PANEL)


def factor_low(planes, ridge):
    rows = planes.shape[1]
    return pl.pallas_call(
        low_kernel,
        out_shape=(jax.ShapeDtypeStruct((PAIR, PAIR + EXTRA), F32), jax.ShapeDtypeStruct(PANELS_SHAPE, F32)),
        in_specs=[HB, SM],
        out_specs=(VM, VM),
        scratch_shapes=[pltpu.VMEM((2, rows, BLOCK), F32), pltpu.VMEM((HALF, 2 * HALF), F32), pltpu.VMEM((2, HALF, HALF), F32), pltpu.SemaphoreType.DMA((2,))],
        compiler_params=pltpu.CompilerParams(vmem_limit_bytes=24 * MIB),
        cost_estimate=pl.CostEstimate(flops=40_000_000_000, bytes_accessed=10_000_000, transcendentals=0),
        name="factor_low",
    )(planes, ridge)


def factor_high(planes, ridge, up_low, inv_low, cross):
    rows = planes.shape[1]
    return pl.pallas_call(
        high_kernel,
        out_shape=jax.ShapeDtypeStruct((1, 2 * PAIR), F32),
        in_specs=[HB, SM, VM, VM, VM],
        out_specs=VM,
        scratch_shapes=[
            pltpu.VMEM((2, rows, BLOCK), F32),
            pltpu.VMEM((PAIR, PAIR + EXTRA), F32),
            pltpu.VMEM((PAIR, PAIR + EXTRA), F32),
            pltpu.VMEM(PANELS_SHAPE, F32),
            pltpu.VMEM((HALF, 2 * HALF), F32),
            pltpu.VMEM((2, HALF, HALF), F32),
            pltpu.SemaphoreType.DMA((2,)),
        ],
        compiler_params=pltpu.CompilerParams(vmem_limit_bytes=30 * MIB),
        cost_estimate=pl.CostEstimate(flops=50_000_000_000, bytes_accessed=10_000_000, transcendentals=0),
        name="factor_high",
    )(planes, ridge, up_low, inv_low, cross)


CROSS_ROWS = 2048


def cross_kernel(early, has_pair, has_prev, own, mate_lo, mate_hi, far_c, far_d, *refs):
    out, panel = refs[-2:]
    z = lax.axis_index('tp')
    mate, even, other = z_peers(z)

    def column(index):
        return pl.ds(pl.multiple_of(index * BLOCK, BLOCK), BLOCK)

    @pl.when(pl.program_id(0) == 0)
    def _():
        out[...] = refs[-3][...] if has_prev else jnp.zeros((CROSS_ROWS, BLOCK), F32)
        if has_pair:
            out[2 * PAIR:2 * PAIR + BLOCK] += refs[0][...]

    @pl.when(z == (1 if early else 0))
    def _():
        panel[:, column(z)] = own[...]
        panel[:, column(even)] = far_d[...]
        panel[:, column(other)] = far_c[...]
        panel[:, column(mate)] = mate_lo[...]
        for j in range(2):
            a = j * PAIR
            out[a:a + PAIR] += dot(panel[:, :PAIR], panel[:, PAIR + j * BLOCK:PAIR + (j + 1) * BLOCK], ((0,), (0,)))

    @pl.when(z >= 2)
    def _():
        panel[:, column(z)] = own[...]
        panel[:, column(even)] = far_d[...]
        panel[:, column(other)] = far_c[...]
        panel[:, column(mate)] = mate_hi[...]
        i = 1 if early else 0
        for j in range(2):
            a = j * PAIR + i * BLOCK
            out[a:a + BLOCK] += dot(panel[:, i * BLOCK:(i + 1) * BLOCK], panel[:, PAIR + j * BLOCK:PAIR + (j + 1) * BLOCK], ((0,), (0,)))
        if early:
            out[2 * PAIR:2 * PAIR + BLOCK] += dot(panel[:, PAIR:PAIR + BLOCK], panel[:, PAIR + BLOCK:], ((0,), (0,)))


def cross_gram(early, row0, own, mate_lo, mate_hi, far_c, far_d, prev=None, pair=None):
    rows = far_c.shape[0]
    tile = 256
    steps = rows // tile
    shift = row0 // tile
    near = pl.BlockSpec((tile, BLOCK), lambda i: (i + shift, 0))
    far = pl.BlockSpec((tile, BLOCK), lambda i: (i, 0))
    extras = [a for a in (pair, prev) if a is not None]

    return pl.pallas_call(
        functools.partial(cross_kernel, early, pair is not None, prev is not None),
        out_shape=jax.ShapeDtypeStruct((CROSS_ROWS, BLOCK), F32),
        grid=(steps,),
        in_specs=[near, near, near, far, far] + [pl.BlockSpec(a.shape, lambda i: (0, 0)) for a in extras],
        out_specs=pl.BlockSpec((CROSS_ROWS, BLOCK), lambda i: (0, 0)),
        scratch_shapes=[pltpu.VMEM((tile, 2 * PAIR), F32)],
        compiler_params=pltpu.CompilerParams(dimension_semantics=("arbitrary",), vmem_limit_bytes=24 * MIB),
        cost_estimate=pl.CostEstimate(flops=rows * 6_000_000, bytes_accessed=rows * 8000, transcendentals=0),
        name="cross_gram",
    )(own, mate_lo, mate_hi, far_c, far_d, *extras)


def pair_kernel(low, count, *refs):
    nears, mates, heads, out = refs[:count], refs[count:2 * count], refs[2 * count:-1], refs[-1]
    z = lax.axis_index('tp')
    r = BLOCK if low else 0

    @pl.when(pl.program_id(0) == 0)
    def _():
        if len(heads) == 1:
            out[...] = heads[0][...]
        elif low:
            out[:BLOCK] = heads[0][...]
            out[BLOCK:PAIR] = jnp.zeros((BLOCK, BLOCK), F32)
            out[PAIR:] = jnp.broadcast_to(heads[1][...], (EXTRA, BLOCK))
        else:
            out[...] = jnp.zeros((BLOCK, BLOCK), F32)

    mine = z < 2 if low else z >= 2
    for odd in range(2):
        @pl.when(mine & (lax.rem(z, 2) == odd))
        def _():
            for near, mate in zip(nears, mates):
                one, two = (mate, near) if odd else (near, mate)
                out[r:r + BLOCK] += dot(one[...], two[...], ((0,), (0,)))


def pair_gram(low, nears, mates, heads):
    rows = mates[0].shape[0]
    tile = 256
    out_rows = PAIR + EXTRA if low else BLOCK
    rolling = pl.BlockSpec((tile, BLOCK), lambda i: (i, 0))
    return pl.pallas_call(
        functools.partial(pair_kernel, low, len(nears)),
        out_shape=jax.ShapeDtypeStruct((out_rows, BLOCK), F32),
        grid=(rows // tile,),
        in_specs=[rolling] * (2 * len(nears)) + [pl.BlockSpec(h.shape, lambda i: (0, 0)) for h in heads],
        out_specs=pl.BlockSpec((out_rows, BLOCK), lambda i: (0, 0)),
        compiler_params=pltpu.CompilerParams(dimension_semantics=("arbitrary",), vmem_limit_bytes=24 * MIB),
        cost_estimate=pl.CostEstimate(flops=rows * 3_000_000 * len(nears), bytes_accessed=rows * 6000, transcendentals=0),
        name="pair_gram",
    )(*nears, *mates, *heads)


def residual_kernel(steps, design, x_ref, target, out, fits, send_sem, recv_sem):
    z, dp = lax.axis_index('tp'), lax.axis_index('dp')
    i = pl.program_id(0)
    tile = design.shape[0]
    peers = [{'tp': p, 'dp': dp} for p in z_peers(z)]

    @pl.when(i == 0)
    def _():
        barrier = pltpu.get_barrier_semaphore()
        for peer in peers:
            pl.semaphore_signal(barrier, inc=1, device_id=peer, device_id_type=MESH)
        pl.semaphore_wait(barrier, 3)

    x = [x_ref[0:1, pl.ds(pl.multiple_of(z * BLOCK + c * HALF, HALF), HALF)] for c in range(BLOCK // HALF)]
    rows = []
    for r in range(tile // HALF):
        t = sum(design[r * HALF:(r + 1) * HALF, c * HALF:(c + 1) * HALF] * x[c] for c in range(BLOCK // HALF))
        rows.append(jnp.sum(t.T, axis=0, keepdims=True))
    per = tile // HALF
    fits[0, pl.ds(pl.multiple_of(i * per, per), per), :] = jnp.concatenate(rows, axis=0)

    @pl.when(i == steps - 1)
    def _():
        copies = []
        for j, peer in enumerate(peers):
            copy = pltpu.make_async_remote_copy(src_ref=fits.at[0], dst_ref=fits.at[j + 1], send_sem=send_sem.at[j], recv_sem=recv_sem.at[j], device_id=peer, device_id_type=MESH)
            copy.start()
            copies.append(copy)
        for copy in copies:
            copy.wait()
        lo = jnp.where(z % 2 == 0, fits[0] + fits[1], fits[1] + fits[0])
        hi = jnp.where(z % 2 == 0, fits[2] + fits[3], fits[3] + fits[2])
        out[...] = target[...] - (lo + hi)


def residual(design_blk, x_row, target_tile):
    rows = design_blk.shape[0]
    tile = 1024
    steps = rows // tile
    whole = pl.BlockSpec(target_tile.shape, lambda i: (0, 0))
    return pl.pallas_call(
        functools.partial(residual_kernel, steps),
        out_shape=jax.ShapeDtypeStruct(target_tile.shape, F32),
        grid=(steps,),
        in_specs=[pl.BlockSpec((tile, BLOCK), lambda i: (i, 0)), pl.BlockSpec(x_row.shape, lambda i: (0, 0)), whole],
        out_specs=whole,
        scratch_shapes=[pltpu.VMEM((4,) + target_tile.shape, F32), pltpu.SemaphoreType.DMA((3,)), pltpu.SemaphoreType.DMA((3,))],
        compiler_params=pltpu.CompilerParams(collective_id=3, has_side_effects=True, dimension_semantics=("arbitrary",), vmem_limit_bytes=24 * MIB),
        cost_estimate=pl.CostEstimate(flops=6_000_000_000, bytes_accessed=13_000_000, transcendentals=0),
        name="residual",
    )(design_blk, x_row, target_tile)


EDGES = (0, 512, 1280, 2048)


def solution(mesh):
    col_ways, row_ways = mesh.shape['tp'], mesh.shape['dp']

    def swap(block, one, two):
        pairs = [(s * row_ways + d, t * row_ways + d) for s, t in ((one, two), (two, one)) for d in range(row_ways)]
        return lax.ppermute(block, ('tp', 'dp'), pairs)

    def local_fit(design_blk, target_blk, ridge):
        rows_dev, _ = design_blk.shape
        quarter_rows = rows_dev // col_ways
        z = lax.axis_index('tp')

        def piece(array, index):
            return lax.dynamic_slice_in_dim(array, index * quarter_rows, quarter_rows)

        to_mate = piece(design_blk, z ^ 1)
        to_mate, design_b = lax.optimization_barrier((to_mate, design_blk))
        low_a = swap(to_mate, 0, 1)
        to_third, to_even, own = piece(design_b, z ^ 3), piece(design_b, z ^ 2), piece(design_b, z)
        low_b = swap(to_third, 0, 1)
        near_c = swap(to_third, 1, 2)
        near_d = swap(to_even, 1, 3)
        high_a = swap(to_mate, 2, 3)
        to_third_b, to_even_b, own = lax.optimization_barrier((to_third, to_even, own))
        chunks = [(to_third_b[i:j], to_even_b[i:j]) for i, j in zip(EDGES, EDGES[1:])]
        own_gram = dot(design_b, design_b, ((0,), (0,)))
        moment = dot(target_blk[None, :], design_b)
        part = pair_gram(True, (own,), (low_a,), (own_gram, moment))
        low_a, low_b, near_c, near_d, part, chunks = lax.optimization_barrier(
            (low_a, low_b, near_c, near_d, part, chunks))
        far_c, far_d = [], []

        def send_late(pieces):
            far_c.append(swap(pieces[0], 0, 3))
            far_d.append(swap(pieces[1], 0, 2))

        send_late(chunks[0])
        part = pair_gram(True, (to_even,), (low_b,), (part,))
        mine = stack_planes(part, 1)
        mine, late_b, chunks = lax.optimization_barrier((mine, to_third, chunks))
        send_late(chunks[1])
        high_b = swap(late_b, 2, 3)
        send_late(chunks[2])
        planes = spread_planes(mine, 2)
        ridge_cell = jnp.reshape(ridge, (1, 1))
        up_low, inv_low = factor_low(planes, ridge_cell)
        own_b, near_c, up_low = lax.optimization_barrier((own, near_c, up_low))
        cross = cross_gram(True, 0, own_b, low_a, high_a, near_c, near_d)
        cross = cross_gram(False, EDGES[0], own_b, low_a, high_a, far_c[0], far_d[0], cross)
        cross = cross_gram(False, EDGES[1], own_b, low_a, high_a, far_c[1], far_d[1], cross)
        high_b, cross = lax.optimization_barrier((high_b, cross))
        pair_high = pair_gram(False, (to_even,), (high_b,), ())
        cross = cross_gram(False, EDGES[2], own_b, low_a, high_a, far_c[2], far_d[2], cross, pair_high)
        cross = sum_all(cross, 4)
        x_row = factor_high(planes, ridge_cell, up_low, inv_low, cross)
        left = residual(design_b, x_row, jnp.reshape(target_blk, (rows_dev // HALF, HALF)))
        return x_row[0], jnp.reshape(left, (rows_dev,))

    return jax.shard_map(local_fit, mesh=mesh, in_specs=(P('dp', 'tp'), P('dp'), P()), out_specs=(P(), P('dp')), check_vma=False)
```

time: 532 us -> 477 us (0.90)
  waiting for transfers between devices: 225 us -> 104 us
  starting transfers between devices: 7.11 us -> 48.2 us
  Pallas kernels: 222 us -> 262 us
  matrix products: 48.1 us -> 30.6 us
    ppermute x4 -> x12, waiting for transfers between devices: 225 us -> 104 us  [swap(): return lax.ppermute(block, ('tp', 'dp'), pairs)]
    pallas_call x4 -> x10, Pallas kernels: 128 us -> 170 us  [the longest x3 115 us: comm_call(): pl.pallas_call(functools.partial(body, rows), out_shape=jax.ShapeDtypeStr...]
    ppermute x4 -> x12, starting transfers between devices: 7.11 us -> 48.2 us  [swap(): return lax.ppermute(block, ('tp', 'dp'), pairs)]
    dot_general x4 -> x2, matrix products: 48.1 us -> 30.6 us  [dot(): lax.dot_general(a, b, (dims, ((), ())), precision=HIGHEST, preferred_elem...]
    slice x0 -> x3, local copies, waits for them, and re-layouts: none -> 8.57 us  [the longest x2 6.51 us: local_fit(): to_even_b[i:j]]
    dynamic_slice x1 -> x2, local copies, waits for them, and re-layouts: 8.8 us -> 10.8 us  [piece(): return lax.dynamic_slice_in_dim(array, index * quarter_rows, quarter_rows)]
  transfers between devices with their start and end apart: 4 -> 12, of which waited for: 2 -> 4; matrix products, arithmetic and copies ran while one was open for 10% -> 10% of each run, Pallas kernels for 2% -> 31%
where the time goes in v3:
time: 477 us; the launch traced here: 472 us
  Pallas kernels  262 us (55%)
  waiting for transfers between devices  104 us (22%)
  starting transfers between devices  48.2 us (10%)
  matrix products  30.6 us (6%)
  local copies, waits for them, and re-layouts  24.6 us (5%)
    pallas_call x3, Pallas kernels, comm_call(): pl.pallas_call(functools.partial(body, rows), out_shape=jax.ShapeDtypeStr...  115 us
    ppermute x12, waiting for transfers between devices, swap(): return lax.ppermute(block, ('tp', 'dp'), pairs)  104 us
    ppermute x12, starting transfers between devices, swap(): return lax.ppermute(block, ('tp', 'dp'), pairs)  48.2 us
    pallas_call x1, Pallas kernels, factor_high(): pl.pallas_call(high_kernel, out_shape=jax.ShapeDtypeStruct((1, 2 * PAIR),...  47.3 us
    pallas_call x1, Pallas kernels, factor_low(): pl.pallas_call(low_kernel, out_shape=(jax.ShapeDtypeStruct((PAIR, PAIR +...  35.5 us
    pallas_call x4, Pallas kernels, cross_gram(): pl.pallas_call(functools.partial(cross_kernel, early, pair is not None, p...  33.4 us
    dot_general x2, matrix products, dot(): lax.dot_general(a, b, (dims, ((), ())), precision=HIGHEST, preferred_elem...  30.6 us
    pallas_call x3, Pallas kernels, pair_gram(): pl.pallas_call(functools.partial(pair_kernel, low, len(nears)), out_shape...  21.5 us
  transfers between devices with their start and end apart: 12, of which 4 were waited for; matrix products, arithmetic and copies ran while one was open for 10% of the time, Pallas kernels for 31%

profile of v3, /device:TPU:0, one launch (start us, length us, event | category | flops | bytes accessed | tf_op | source)
XLA Modules:
  0.0 471.6 jit_solution(14713505871834602583)
XLA Ops:
  4.4 4.9 %collective-permute-start = (f32[2048,384]{1,0:T(8,128)}, f32[2048,384]{1,0:T(8,128)}, u32[]{:S(2)}, u32[]{:S(2)}) collective-permute-start(f32[2048,384]{1,0:T(8,128)} %constant_dynamic-slice_fusion.3), channel_id=1, source_target_pairs={{0,8},{1,9},{2,10},{3,11},{4,12},{5,13},{6,14},{7,15},{8,0},{9,1},... | collective-permute-start | bytes 9437192 | tf_op jit(solution)/shard_map/ppermute | solution.py:554
  9.3 7.1 %constant_dynamic-slice_fusion = (f32[2048,384]{1,0:T(8,128)S(1)}, f32[2048,384]{1,0:T(8,128)}, f32[2048,384]{1,0:T(8,128)}) fusion(f32[8192,384]{1,0:T(8,128)} %design, s32[]{:T(128)S(6)} %select_n.15, s32[]{:T(128)S(6)} %select_n.14, s32[]{:T(128)S(6)} %select_n.13), kind=kLoop, calls=%fused_computation | loop fusion | bytes 18874380 | tf_op jit(solution)/shard_map/dynamic_slice | solution.py:562
  31.8 4.3 fusion
  36.1 9.8 %fusion.3.refs_3_ = f32[1,384]{1,0:T(1,128)S(1)} fusion(f32[8192,384]{1,0:T(8,128)} %design, f32[8192,1]{0,1:T(1,128)S(1)} %bitcast.12), kind=kOutput, calls=%fused_computation.7 | convolution fusion | flops 37748736 | bytes 12617216 | tf_op jit(solution)/shard_map/dot_general | solution.py:18
  45.9 20.8 %fusion.2.refs_2_ = f32[384,384]{1,0:T(8,128)S(1)} fusion(f32[8192,384]{1,0:T(8,128)S(1)} %bitcast.11), kind=kOutput, calls=%fused_computation.6 | convolution fusion | flops 14495514624 | bytes 13172736 | tf_op jit(solution)/shard_map/dot_general | solution.py:18
  66.8 11.8 %collective-permute-done.refs_1_.mate_lo = f32[2048,384]{1,0:T(8,128)} collective-permute-done((f32[2048,384]{1,0:T(8,128)}, f32[2048,384]{1,0:T(8,128)}, u32[]{:S(2)}, u32[]{:S(2)}) %collective-permute-start) | collective-permute-done | bytes 3145760 | tf_op jit(solution)/shard_map/ppermute | solution.py:554
  78.6 8.4 %pair_gram.3.refs_2_ = f32[896,384]{1,0:T(8,128)S(1)} custom-call(f32[2048,384]{1,0:T(8,128)S(1)} %get-tuple-element.49.refs_0_.own, f32[2048,384]{1,0:T(8,128)} %collective-permute-done.refs_1_.mate_lo, f32[384,384]{1,0:T(8,128)S(1)} %fusion.2.refs_2_, f32[1,384]{1,0:T(1,128)S(1)} %fusion.3.refs_3_), custom_call_target="tpu_custom_call" | custom-call | flops 6144000000 | bytes 12288000 | tf_op jit(solution)/shard_map/pair_gram/pallas_call | solution.py:481
  87.0 58.2 %collective-permute-done.1.refs_1_ = f32[2048,384]{1,0:T(8,128)} collective-permute-done((f32[2048,384]{1,0:T(8,128)}, f32[2048,384]{1,0:T(8,128)}, u32[]{:S(2)}, u32[]{:S(2)}) %collective-permute-start.1) | collective-permute-done | bytes 3145760 | tf_op jit(solution)/shard_map/ppermute | solution.py:554
  145.1 8.9 %pair_gram.4.part = f32[896,384]{1,0:T(8,128)S(1)} custom-call(f32[2048,384]{1,0:T(8,128)} %get-tuple-element.35.refs_0_, f32[2048,384]{1,0:T(8,128)} %collective-permute-done.1.refs_1_, f32[896,384]{1,0:T(8,128)S(1)} %pair_gram.3.refs_2_), custom_call_target="tpu_custom_call" | custom-call | flops 6144000000 | bytes 12288000 | tf_op jit(solution)/shard_map/pair_gram/pallas_call | solution.py:481
  154.1 37.8 %shard_map.50.mine = f32[4,112,384]{2,1,0:T(8,128)S(1)} custom-call(f32[896,384]{1,0:T(8,128)S(1)} %pair_gram.4.part), custom_call_target="tpu_custom_call" | custom-call | flops 1792000 | bytes 80000000 | tf_op jit(solution)/shard_map/pallas_call | solution.py:267
  201.5 27.4 %shard_map.51.planes = f32[4,896,384]{2,1,0:T(8,128)S(1)} custom-call(f32[4,112,384]{2,1,0:T(8,128)S(1)} %shard_map.50.mine), custom_call_target="tpu_custom_call" | custom-call | flops 1792000 | bytes 80000000 | tf_op jit(solution)/shard_map/pallas_call | solution.py:267
  229.0 35.5 %factor_low.1 = (f32[768,896]{1,0:T(8,128)S(1)}, f32[3,256,256]{2,1,0:T(8,128)S(1)}) custom-call(f32[4,896,384]{2,1,0:T(8,128)S(1)} %shard_map.51.planes, f32[1,1]{1,0:T(1,128)} %bitcast.8.ridge), custom_call_target="tpu_custom_call" | custom-call | flops 40000000000 | bytes 10000000 | tf_op jit(solution)/shard_map/factor_low/pallas_call | solution.py:354
  264.5 7.4 %collective-permute-start.9 = (f32[768,384]{1,0:T(8,128)}, f32[768,384]{1,0:T(8,128)S(1)}, u32[]{:S(2)}, u32[]{:S(2)}) collective-permute-start(f32[768,384]{1,0:T(8,128)} %get-tuple-element.55), channel_id=1, source_target_pairs={{0,16},{1,17},{2,18},{3,19},{4,20},{5,21},{6,22},{7,23},{16,0},{17... | collective-permute-start | bytes 3538952 | tf_op jit(solution)/shard_map/ppermute | solution.py:554
  271.9 6.4 %cross_gram.4.refs_0_ = f32[2048,384]{1,0:T(8,128)S(1)} custom-call(f32[2048,384]{1,0:T(8,128)S(1)} %get-tuple-element.49.refs_0_.own, f32[2048,384]{1,0:T(8,128)} %collective-permute-done.refs_1_.mate_lo, f32[2048,384]{1,0:T(8,128)} %collective-permute-done.4.mate_hi, f32[2048,384]{1,0:T(8,128)} %collective-permute-done.2.far_c, ...), custom_call_target="tpu_custom_call" | custom-call | flops 12288000000 | bytes 16384000 | tf_op jit(solution)/shard_map/cross_gram/pallas_call | solution.py:438
  278.3 13.2 %collective-permute-start.5 = (f32[768,384]{1,0:T(8,128)S(1)}, f32[768,384]{1,0:T(8,128)S(1)}, u32[]{:S(2)}, u32[]{:S(2)}) collective-permute-start(f32[768,384]{1,0:T(8,128)S(1)} %get-tuple-element.51), channel_id=1, source_target_pairs={{0,24},{1,25},{2,26},{3,27},{4,28},{5,29},{6,30},{7,31},{24,0},{25... | collective-permute-start | bytes 3538952 | tf_op jit(solution)/shard_map/ppermute | solution.py:554
  294.2 7.0 %cross_gram.5.refs_0_ = f32[2048,384]{1,0:T(8,128)S(1)} custom-call(f32[2048,384]{1,0:T(8,128)S(1)} %get-tuple-element.49.refs_0_.own, f32[2048,384]{1,0:T(8,128)} %collective-permute-done.refs_1_.mate_lo, f32[2048,384]{1,0:T(8,128)} %collective-permute-done.4.mate_hi, f32[512,384]{1,0:T(8,128)S(1)} %collective-permute-done.10.far_c, ...), custom_call_target="tpu_custom_call" | custom-call | flops 3072000000 | bytes 4096000 | tf_op jit(solution)/shard_map/cross_gram/pallas_call | solution.py:438
  301.2 9.8 %cross_gram.6.refs_1_ = f32[2048,384]{1,0:T(8,128)S(1)} custom-call(f32[2048,384]{1,0:T(8,128)S(1)} %get-tuple-element.49.refs_0_.own, f32[2048,384]{1,0:T(8,128)} %collective-permute-done.refs_1_.mate_lo, f32[2048,384]{1,0:T(8,128)} %collective-permute-done.4.mate_hi, f32[768,384]{1,0:T(8,128)S(1)} %collective-permute-done.8.far_c, ...), custom_call_target="tpu_custom_call" | custom-call | flops 4608000000 | bytes 6144000 | tf_op jit(solution)/shard_map/cross_gram/pallas_call | solution.py:438
  315.3 16.2 %collective-permute-done.5.far_c = f32[768,384]{1,0:T(8,128)S(1)} collective-permute-done((f32[768,384]{1,0:T(8,128)S(1)}, f32[768,384]{1,0:T(8,128)S(1)}, u32[]{:S(2)}, u32[]{:S(2)}) %collective-permute-start.5) | collective-permute-done | bytes 1179680 | tf_op jit(solution)/shard_map/ppermute | solution.py:554
  331.5 17.5 %collective-permute-done.6.far_d = f32[768,384]{1,0:T(8,128)S(1)} collective-permute-done((f32[768,384]{1,0:T(8,128)S(1)}, f32[768,384]{1,0:T(8,128)S(1)}, u32[]{:S(2)}, u32[]{:S(2)}) %collective-permute-start.6) | collective-permute-done | bytes 1179680 | tf_op jit(solution)/shard_map/ppermute | solution.py:554
  349.0 10.2 %cross_gram.7.part = f32[2048,384]{1,0:T(8,128)S(1)} custom-call(f32[2048,384]{1,0:T(8,128)S(1)} %get-tuple-element.49.refs_0_.own, f32[2048,384]{1,0:T(8,128)} %collective-permute-done.refs_1_.mate_lo, f32[2048,384]{1,0:T(8,128)} %collective-permute-done.4.mate_hi, f32[768,384]{1,0:T(8,128)S(1)} %collective-permute-done.5.far_c, ...), custom_call_target="tpu_custom_call" | custom-call | flops 4608000000 | bytes 6144000 | tf_op jit(solution)/shard_map/cross_gram/pallas_call | solution.py:438
  359.2 50.2 %shard_map.52.cross = f32[1,2048,384]{2,1,0:T(8,128)S(1)} custom-call(f32[2048,384]{1,0:T(8,128)S(1)} %cross_gram.7.part), custom_call_target="tpu_custom_call" | custom-call | flops 4096000 | bytes 80000000 | tf_op jit(solution)/shard_map/pallas_call | solution.py:267
  409.5 47.3 %factor_high.1.x_ref = f32[1,1536]{1,0:T(1,128)S(1)} custom-call(f32[4,896,384]{2,1,0:T(8,128)S(1)} %shard_map.51.planes, f32[1,1]{1,0:T(1,128)} %bitcast.9.ridge, f32[768,896]{1,0:T(8,128)S(1)} %get-tuple-element.47.up_low, f32[3,256,256]{2,1,0:T(8,128)S(1)} %get-tuple-element.48.inv_low, f32[1,2048,384]{2,1,0:T(8,128)S(1)} %shard_map.52.cross), custom_call_target="tpu_custom_call" | custom-call | flops 49999998976 | bytes 10000000 | tf_op jit(solution)/shard_map/factor_high/pallas_call | solution.py:368
  457.5 4.6 copy-done
  462.0 8.8 %residual.1 = f32[64,128]{1,0:T(8,128)S(1)} custom-call(f32[8192,384]{1,0:T(8,128)S(1)} %copy-done, f32[1,1536]{1,0:T(1,128)S(1)} %factor_high.1.x_ref, f32[64,128]{1,0:T(8,128)S(1)} %bitcast.13), custom_call_target="tpu_custom_call" | custom-call | flops 6000000000 | bytes 13000000 | tf_op jit(solution)/shard_map/residual/pallas_call | solution.py:533
  (35 shorter events, 36.3 us)
Async XLA Ops:
  4.4 74.2 %collective-permute-start = (f32[2048,384]{1,0:T(8,128)}, f32[2048,384]{1,0:T(8,128)}, u32[]{:S(2)}, u32[]{:S(2)}) collective-permute-start(f32[2048,384]{1,0:T(8,128)} %constant_dynamic-slice_fusion.3), channel_id=1, source_target_pairs={{0,8},{1,9},{2,10},{3,11},{4,12},{5,13},{6,14},{7,15},{8,0},{9,1},... | collective-permute-start | bytes 9437192 | tf_op jit(solution)/shard_map/ppermute | solution.py:554
  16.4 70.5 %collective-permute-start.2 = (f32[2048,384]{1,0:T(8,128)}, f32[2048,384]{1,0:T(8,128)}, u32[]{:S(2)}, u32[]{:S(2)}) collective-permute-start(f32[2048,384]{1,0:T(8,128)} %get-tuple-element.53), channel_id=1, source_target_pairs={{8,16},{9,17},{10,18},{11,19},{12,20},{13,21},{14,22},{15,23},{16,... | collective-permute-start | bytes 9437192 | tf_op jit(solution)/shard_map/ppermute | solution.py:554
  18.7 126.4 %collective-permute-start.1 = (f32[2048,384]{1,0:T(8,128)}, f32[2048,384]{1,0:T(8,128)}, u32[]{:S(2)}, u32[]{:S(2)}) collective-permute-start(f32[2048,384]{1,0:T(8,128)} %get-tuple-element.53), channel_id=1, source_target_pairs={{0,8},{1,9},{2,10},{3,11},{4,12},{5,13},{6,14},{7,15},{8,0},{9,1},... | collective-permute-start | bytes 9437192 | tf_op jit(solution)/shard_map/ppermute | solution.py:554
  22.2 123.0 %collective-permute-start.3 = (f32[2048,384]{1,0:T(8,128)}, f32[2048,384]{1,0:T(8,128)}, u32[]{:S(2)}, u32[]{:S(2)}) collective-permute-start(f32[2048,384]{1,0:T(8,128)} %get-tuple-element.35.refs_0_), channel_id=1, source_target_pairs={{8,24},{9,25},{10,26},{11,27},{12,28},{13,29},{14,30},{15,31},{24,... | collective-permute-start | bytes 9437192 | tf_op jit(solution)/shard_map/ppermute | solution.py:554
  24.5 240.0 %collective-permute-start.4 = (f32[2048,384]{1,0:T(8,128)}, f32[2048,384]{1,0:T(8,128)}, u32[]{:S(2)}, u32[]{:S(2)}) collective-permute-start(f32[2048,384]{1,0:T(8,128)} %constant_dynamic-slice_fusion.3), channel_id=1, source_target_pairs={{16,24},{17,25},{18,26},{19,27},{20,28},{21,29},{22,30},{23,31},{2... | collective-permute-start | bytes 9437192 | tf_op jit(solution)/shard_map/ppermute | solution.py:554
  29.6 16.3 %slice-start = ((s8[12582912]{0:T(1024)(128)(4,1)}), s8[4194304]{0:T(1024)(128)(4,1)S(1)}, s32[]{:S(2)}) async-start(s8[12582912]{0:T(1024)(128)(4,1)} %bitcast.10), calls=%async_computation | async-start | bytes 8388608
  31.8 4.3 copy-start.1
  31.8 14.1 %slice-start.1 = ((s8[12582912]{0:T(1024)(128)(4,1)}), s8[4194304]{0:T(1024)(128)(4,1)S(1)}, s32[]{:S(2)}) async-start(s8[12582912]{0:T(1024)(128)(4,1)} %bitcast.10), calls=%async_computation.1 | async-start | bytes 8388608
  36.1 9.8 %slice-start.2 = ((s8[12582912]{0:T(1024)(128)(4,1)}), s8[4194304]{0:T(1024)(128)(4,1)S(1)}, s32[]{:S(2)}) async-start(s8[12582912]{0:T(1024)(128)(4,1)} %bitcast.10), calls=%async_computation.2 | async-start | bytes 8388608
  191.9 86.4 %collective-permute-start.10 = (f32[512,384]{1,0:T(8,128)}, f32[512,384]{1,0:T(8,128)S(1)}, u32[]{:S(2)}, u32[]{:S(2)}) collective-permute-start(f32[512,384]{1,0:T(8,128)} %slice.18), channel_id=1, source_target_pairs={{0,24},{1,25},{2,26},{3,27},{4,28},{5,29},{6,30},{7,31},{24,0},{25... | collective-permute-start | bytes 2359304 | tf_op jit(solution)/shard_map/ppermute | solution.py:554
  195.7 95.8 %collective-permute-start.11 = (f32[512,384]{1,0:T(8,128)}, f32[512,384]{1,0:T(8,128)S(1)}, u32[]{:S(2)}, u32[]{:S(2)}) collective-permute-start(f32[512,384]{1,0:T(8,128)} %slice.19), channel_id=1, source_target_pairs={{0,16},{1,17},{2,18},{3,19},{4,20},{5,21},{6,22},{7,23},{16,0},{17... | collective-permute-start | bytes 2359304 | tf_op jit(solution)/shard_map/ppermute | solution.py:554
  197.7 103.5 %collective-permute-start.8 = (f32[768,384]{1,0:T(8,128)}, f32[768,384]{1,0:T(8,128)S(1)}, u32[]{:S(2)}, u32[]{:S(2)}) collective-permute-start(f32[768,384]{1,0:T(8,128)} %get-tuple-element.54), channel_id=1, source_target_pairs={{0,24},{1,25},{2,26},{3,27},{4,28},{5,29},{6,30},{7,31},{24,0},{25... | collective-permute-start | bytes 3538952 | tf_op jit(solution)/shard_map/ppermute | solution.py:554
  200.7 110.4 %collective-permute-start.7 = (f32[2048,384]{1,0:T(8,128)}, f32[2048,384]{1,0:T(8,128)S(1)}, u32[]{:S(2)}, u32[]{:S(2)}) collective-permute-start(f32[2048,384]{1,0:T(8,128)} %get-tuple-element.53), channel_id=1, source_target_pairs={{16,24},{17,25},{18,26},{19,27},{20,28},{21,29},{22,30},{23,31},{2... | collective-permute-start | bytes 9437192 | tf_op jit(solution)/shard_map/ppermute | solution.py:554
  264.5 36.6 %collective-permute-start.9 = (f32[768,384]{1,0:T(8,128)}, f32[768,384]{1,0:T(8,128)S(1)}, u32[]{:S(2)}, u32[]{:S(2)}) collective-permute-start(f32[768,384]{1,0:T(8,128)} %get-tuple-element.55), channel_id=1, source_target_pairs={{0,16},{1,17},{2,18},{3,19},{4,20},{5,21},{6,22},{7,23},{16,0},{17... | collective-permute-start | bytes 3538952 | tf_op jit(solution)/shard_map/ppermute | solution.py:554
  278.3 53.2 %collective-permute-start.5 = (f32[768,384]{1,0:T(8,128)S(1)}, f32[768,384]{1,0:T(8,128)S(1)}, u32[]{:S(2)}, u32[]{:S(2)}) collective-permute-start(f32[768,384]{1,0:T(8,128)S(1)} %get-tuple-element.51), channel_id=1, source_target_pairs={{0,24},{1,25},{2,26},{3,27},{4,28},{5,29},{6,30},{7,31},{24,0},{25... | collective-permute-start | bytes 3538952 | tf_op jit(solution)/shard_map/ppermute | solution.py:554
  291.5 57.5 %collective-permute-start.6 = (f32[768,384]{1,0:T(8,128)S(1)}, f32[768,384]{1,0:T(8,128)S(1)}, u32[]{:S(2)}, u32[]{:S(2)}) collective-permute-start(f32[768,384]{1,0:T(8,128)S(1)} %get-tuple-element.52), channel_id=1, source_target_pairs={{0,16},{1,17},{2,18},{3,19},{4,20},{5,21},{6,22},{7,23},{16,0},{17... | collective-permute-start | bytes 3538952 | tf_op jit(solution)/shard_map/ppermute | solution.py:554
  409.5 48.0 %copy-start.2 = (f32[8192]{0:T(1024)S(1)}, f32[8192]{0:T(1024)}, u32[]{:S(2)}) copy-start(f32[8192]{0:T(1024)} %param.4) | copy-start | bytes 98308
  457.5 4.6 copy-start
